TPU v7x, 8 devices: a whole 2x2x1 slice. The times are simulated.
8 devices in a mesh: replica: 2 (over z, y), model: 4 (over x, core).
Axes of the slice: x: 2, y: 2, z: 1, core: 2. Of those that a mesh axis runs over, the one named last changes fastest.
Arguments:
- prompt: bfloat16 [128, 128, 3072], P('replica', 'model'), parts along dimension 0
- lengths: int32 [128], P('replica'), parts along dimension 0
- new_tok: bfloat16 [128, 3072], P('replica'), parts along dimension 0
- norm_attn: bfloat16 [1, 3072], replicated
- w_q: bfloat16 [1, 3072, 3072], P(None, None, 'model')
- w_k: bfloat16 [1, 3072, 1024], P(None, None, 'model')
- w_v: bfloat16 [1, 3072, 1024], P(None, None, 'model')
- w_o: bfloat16 [1, 3072, 3072], P(None, 'model')
- norm_mlp: bfloat16 [1, 3072], replicated
- w_gate: bfloat16 [1, 3072, 8192], P(None, None, 'model')
- w_up: bfloat16 [1, 3072, 8192], P(None, None, 'model')
- w_down: bfloat16 [1, 8192, 3072], P(None, 'model')
Outputs:
- output 1: bfloat16 [128, 3072], P('replica'), parts along dimension 0
- output 2: bfloat16 [128, 3072], P('replica'), parts along dimension 0
- output 3: bfloat16 [1, 128, 129, 8, 128], P(None, 'replica', None, 'model'), parts along dimension 1
- output 4: bfloat16 [1, 128, 129, 8, 128], P(None, 'replica', None, 'model'), parts along dimension 1
There are 2 independent parts. A program takes and returns all parts, laid end to end along the dimension named above; an argument that names none is the same for every part.
All inputs are finite; a program needn't handle non-finite values.
Results may differ from a plain program's by a relative error of at most 0.0108268.
Values are sent between devices in bfloat16 or wider.
A program may use at most 1 GiB of HBM per device.

v0:
```python
import functools

import jax
import jax.numpy as jnp
from jax import lax
from jax.experimental import pallas as pl
from jax.experimental.pallas import tpu as pltpu
from jax.sharding import PartitionSpec as P

HEAD_DIM = 128
NEG_BIG = -1e30
MESH = pl.DeviceIdType.MESH
F32 = jnp.float32
BF16 = jnp.bfloat16

NB = 64
SEQ_LOC = 32
D = 3072
FF = 2048
QW = 768
CH = 16
NCH = NB // CH
ROWS = CH * SEQ_LOC
WCH = 4
WROWS = D // WCH


def dot32(lhs, rhs):
    return jnp.dot(lhs, rhs, preferred_element_type=F32)


def rotate_tables(positions):
    half = HEAD_DIM // 2
    inv_freq = 10000.0 ** (-2.0 * jnp.arange(half, dtype=F32) / HEAD_DIM)
    angles = positions.astype(F32)[:, None] * inv_freq
    cos_tab, sin_tab = jnp.cos(angles), jnp.sin(angles)
    return jnp.concatenate([cos_tab, cos_tab], 1), jnp.concatenate([-sin_tab, sin_tab], 1)


def kernel(lens, tab_c, tab_s, rot_c, rot_s, g_attn, g_mlp, new_tok,
           prompt, w_q, w_k, w_v, w_o, w_g, w_u, w_d,
           o_hid, o_kv, o_new,
           buf_a, buf_b, buf_c, kv, stage, flat, q_buf, k_buf, v_buf, a_buf, att,
           sel_r1, sel_r2, hid, normed, part, r1, r2, n2, mid, hid2, out_buf, knv,
           ld_p, ld_w, ld_big, st_sem,
           wp_s, wp_r, wx_s, wx_r, wfx_s, wfx_r, wy_s, wy_r, wfy_s, wfy_r,
           sel_s, sel_r, kv_s, kv_r, ar_s, ar_r):
    y = lax.axis_index("replica")
    m = lax.axis_index("model")
    c = lax.rem(m, 2)
    x = m // 2
    xs_m = lax.rem(m + 2, 4)
    xo_m = 3 - m
    pt_m = m + 1 - 2 * c
    xs, xo, pt, yp = (y, xs_m), (y, xo_m), (y, pt_m), (1 - y, m)

    def remote(src, dst, ssem, rsem, dev):
        return pltpu.make_async_remote_copy(src_ref=src, dst_ref=dst, send_sem=ssem, recv_sem=rsem,
                                            device_id=dev, device_id_type=MESH)

    def load_w(i):
        src = (w_k, w_v)[i]
        return pltpu.make_async_copy(src, buf_b.at[:, pl.ds(pl.multiple_of(m * 512 + i * 256, 256), 256)], ld_w.at[i])

    def load_p(j):
        r = pl.ds(pl.multiple_of(j * ROWS, ROWS), ROWS)
        return pltpu.make_async_copy(prompt.at[r], buf_a.at[r], ld_p.at[j])

    for i in range(2):
        load_w(i).start()
    for j in range(NCH):
        load_p(j).start()
    load_q = pltpu.make_async_copy(w_q, buf_c.at[:, pl.ds(0, QW)], ld_big.at[0])
    load_q.start()

    def load_o(i):
        return pltpu.make_async_copy(w_o.at[:, pl.ds(i * QW, QW)], buf_c.at[pl.ds(i * QW, QW), pl.ds(QW, QW)], ld_big.at[1 + i])

    for i in range(4):
        load_o(i).start()
    load_g = pltpu.make_async_copy(w_g, buf_b, ld_big.at[5])
    load_u = pltpu.make_async_copy(w_u, buf_c, ld_big.at[6])
    load_d = pltpu.make_async_copy(w_d, buf_a, ld_big.at[7])

    barrier = pltpu.get_barrier_semaphore()
    for dev in (xs, xo, pt, yp):
        pl.semaphore_signal(barrier, inc=1, device_id=dev, device_id_type=MESH)
    pl.semaphore_wait(barrier, 4)

    def w_ref(owner, h, r):
        return buf_b.at[pl.ds(r * WROWS, WROWS), pl.ds(pl.multiple_of(owner * 512 + h * 256, 256), 256)]

    def wx(r):
        ref = w_ref(m, y, r)
        return remote(ref, ref, wx_s.at[r], wx_r.at[r], xs)

    def wfx(r):
        ref = w_ref(xs_m, y, r)
        return remote(ref, ref, wfx_s.at[r], wfx_r.at[r], pt)

    def wy(r):
        ref = w_ref(xs_m, y, r)
        return remote(ref, ref, wy_s.at[r], wy_r.at[r], yp)

    def wfy(r):
        ref = w_ref(xs_m, 1 - y, r)
        return remote(ref, ref, wfy_s.at[r], wfy_r.at[r], pt)

    own = buf_b.at[:, pl.ds(pl.multiple_of(m * 512, 512), 512)]
    wp = remote(own, own, wp_s, wp_r, pt)
    for i in range(2):
        load_w(i).wait()
    for r in range(WCH):
        wx(r).start()
    wp.start()

    def forward_x(r):
        wx(r).wait_recv()
        wfx(r).start()
        wy(r).start()

    def forward_y(r):
        wy(r).wait_recv()
        wfy(r).start()

    gain_a = g_attn[...].astype(F32)
    row_iota = lax.broadcasted_iota(jnp.int32, (SEQ_LOC, 1), 0)

    def norm_prompts(i, carry):
        parts = []
        for t in range(8):
            b = i * 8 + t
            rows = pl.ds(pl.multiple_of(b * SEQ_LOC, SEQ_LOC), SEQ_LOC)
            v = buf_a[rows, :].astype(F32)
            inv = lax.rsqrt(jnp.mean(v * v, axis=-1, keepdims=True) + 1e-5)
            hit = row_iota == lens[b] - 1 - m * SEQ_LOC
            parts.append(jnp.sum(jnp.where(hit, v, 0.0), axis=0, keepdims=True))
            buf_a[rows, :] = (buf_a[rows, :].astype(F32) * inv * gain_a).astype(BF16)
        part[pl.ds(pl.multiple_of(i * 8, 8), 8), :] = jnp.concatenate(parts, axis=0)
        return carry

    per = CH // 8
    for j in range(NCH):
        load_p(j).wait()
        lax.fori_loop(j * per, (j + 1) * per, norm_prompts, 0)

    sel_b = normed.at[pl.ds(0, NB)]
    sel_b[...] = part[0:NB, :].astype(BF16)
    s1 = remote(sel_b, sel_r1, sel_s.at[0], sel_r.at[0], pt)
    s1.start()

    def unit_chunk(owner, h, j):
        col = pl.ds(pl.multiple_of(owner * 512 + h * 256, 256), 256)
        acc = dot32(buf_a[pl.ds(pl.multiple_of(j * ROWS, ROWS), ROWS), :], buf_b[:, col])
        ct, st = tab_c[h], tab_s[h]
        for hd in range(2):
            a = acc[:, hd * HEAD_DIM:(hd + 1) * HEAD_DIM]
            turned = pltpu.roll(a, HEAD_DIM // 2, 1)
            res = a.reshape(CH, SEQ_LOC, HEAD_DIM) * ct[None] + turned.reshape(CH, SEQ_LOC, HEAD_DIM) * st[None]
            flat[pl.ds(hd, ROWS, stride=2), :] = res.reshape(ROWS, HEAD_DIM)
        return flat[...].astype(BF16).reshape(CH, 2 * SEQ_LOC, HEAD_DIM)

    def kv_ref(h, j):
        return kv.at[h, pl.ds(pl.multiple_of(j * CH, CH), CH), pl.ds(pl.multiple_of(m * 64, 64), 64)]

    def kv_send(kind, turn, j):
        dev = (pt, xs, xo)[kind]
        h = y if turn == 0 else 1 - y
        return remote(stage.at[kind, turn, j], kv_ref(h, j), kv_s.at[kind, turn, j], kv_r.at[kind, turn, j], dev)

    def run_unit(kind, turn, j):
        owner = (pt_m, xs_m, xo_m)[kind]
        h = y if turn == 0 else 1 - y
        stage[kind, turn, j] = unit_chunk(owner, h, j)
        kv_send(kind, turn, j).start()

    forward_x(0)

    def own_units(i, carry):
        h, j = i // NCH, lax.rem(i, NCH)
        kv[h, pl.ds(pl.multiple_of(j * CH, CH), CH), pl.ds(pl.multiple_of(m * 64, 64), 64)] = unit_chunk(m, h, j)
        return carry

    lax.fori_loop(0, 2 * NCH, own_units, 0)
    forward_x(1)

    s1.wait()
    sel_b[...] = (sel_b[...].astype(F32) + sel_r1[...].astype(F32)).astype(BF16)
    half = pl.ds(pl.multiple_of(c * 32, 32), 32)
    s2 = remote(normed.at[half], sel_r2, sel_s.at[1], sel_r.at[1], xs)
    s2.start()

    wp.wait_recv()

    def loop_unit(kind, turn):
        def body(j, carry):
            run_unit(kind, turn, j)
            return carry
        lax.fori_loop(0, NCH, body, 0)

    loop_unit(0, 0)
    forward_x(2)
    forward_y(0)
    loop_unit(0, 1)
    forward_x(3)
    loop_unit(1, 0)
    forward_y(1)
    for r in range(WCH):
        wfx(r).wait_recv()
    loop_unit(2, 0)
    forward_y(2)

    s2.wait()
    hid[half, :] = (normed[half, :].astype(F32) + sel_r2[...].astype(F32)).astype(BF16)
    s3 = remote(hid.at[half], hid.at[half], sel_s.at[2], sel_r.at[2], pt)
    s3.start()
    hid[pl.ds(NB, NB), :] = new_tok[...]
    forward_y(3)
    for r in range(WCH):
        wfy(r).wait_recv()

    def last_units(j, carry):
        run_unit(1, 1, j)
        run_unit(2, 1, j)
        return carry

    lax.fori_loop(0, NCH, last_units, 0)
    s3.wait()

    def norm_rows(src, gain):
        v = src.astype(F32)
        inv = lax.rsqrt(jnp.mean(v * v, axis=-1, keepdims=True) + 1e-5)
        return (v * inv * gain).astype(BF16)

    def norm_hid(i, carry):
        rows = pl.ds(pl.multiple_of(i * 32, 32), 32)
        normed[rows, :] = norm_rows(hid[rows, :], gain_a)
        return carry

    lax.fori_loop(0, 4, norm_hid, 0)
    load_q.wait()
    q_buf[...] = jnp.zeros_like(q_buf)
    k_buf[...] = jnp.zeros_like(k_buf)
    v_buf[...] = jnp.zeros_like(v_buf)

    def turn(a, ct, st):
        return (a * ct + pltpu.roll(a, HEAD_DIM // 2, 1) * st).astype(BF16).astype(F32)

    for pair in range(3):
        qs = dot32(normed[...], buf_c[:, pair * 256:(pair + 1) * 256])
        for i in range(2):
            hd = pair * 2 + i
            rot = turn(qs[:, i * HEAD_DIM:(i + 1) * HEAD_DIM], rot_c[...], rot_s[...])
            for t in range(2):
                q_buf[pl.ds(t * 8 + hd, NB, stride=16), :] = rot[t * NB:(t + 1) * NB]
    toks = normed[NB:2 * NB, :]
    k_new = dot32(toks, buf_b[:, pl.ds(pl.multiple_of(m * 512, 256), 256)])
    v_new = dot32(toks, buf_b[:, pl.ds(pl.multiple_of(m * 512 + 256, 256), 256)])
    for g in range(2):
        cols = slice(g * HEAD_DIM, (g + 1) * HEAD_DIM)
        k_g = turn(k_new[:, cols], rot_c[NB:, :], rot_s[NB:, :])
        v_g = v_new[:, cols].astype(BF16).astype(F32)
        flat[pl.ds(g, NB, stride=2), :] = k_g
        flat[pl.ds(2 * NB + g, NB, stride=2), :] = v_g
        for i in range(3):
            rows = pl.ds(8 + 3 * g + i, NB, stride=16)
            k_buf[rows, :] = k_g
            v_buf[rows, :] = v_g
    knv[0] = flat[0:2 * NB, :].astype(BF16)
    knv[1] = flat[2 * NB:4 * NB, :].astype(BF16)
    st_new = pltpu.make_async_copy(knv, o_new, st_sem.at[NCH])
    st_new.start()

    wp.wait_send()
    for r in range(WCH):
        wx(r).wait_send()
        wfx(r).wait_send()
        wy(r).wait_send()
        wfy(r).wait_send()
    load_g.start()
    load_d.start()

    r_io = lax.broadcasted_iota(jnp.int32, (16, 256), 0)
    c_io = lax.broadcasted_iota(jnp.int32, (16, 256), 1)
    same = ((r_io & 7) >= 3) == ((c_io & 1) == 1)
    k_pos = c_io >> 1
    is_new = lax.broadcasted_iota(jnp.int32, (16, 1), 0) >= 8
    scale = HEAD_DIM ** -0.5

    def attend(b):
        rows = pl.ds(pl.multiple_of(b * 16, 16), 16)
        q = q_buf[rows, :]
        s = lax.dot_general(q.astype(BF16), kv[0, b], (((1,), (1,)), ((), ())), preferred_element_type=F32) * scale
        s = jnp.where(same & (k_pos < lens[b]), s, NEG_BIG)
        s_new = jnp.where(is_new, jnp.sum(q * k_buf[rows, :], axis=-1, keepdims=True) * scale, NEG_BIG)
        top = jnp.maximum(jnp.max(s, axis=-1, keepdims=True), s_new)
        p = jnp.exp(s - top)
        p_new = jnp.exp(s_new - top)
        total = jnp.sum(p, axis=-1, keepdims=True) + p_new
        acc = dot32(p.astype(BF16), kv[1, b]) + p_new * v_buf[rows, :]
        a_buf[rows, :] = acc / total

    def attend_four(i, carry):
        for t in range(4):
            attend(i * 4 + t)
        return carry

    def store_kv(j):
        r = pl.ds(j * CH, CH)
        return pltpu.make_async_copy(kv.at[:, r], o_kv.at[:, r], st_sem.at[j])

    for j in range(NCH):
        for kind in range(3):
            for tn in range(2):
                kv_send(kind, tn, j).wait_recv()
        store_kv(j).start()
        lax.fori_loop(j * (CH // 4), (j + 1) * (CH // 4), attend_four, 0)

    for hd in range(6):
        for t in range(2):
            att[t * NB:(t + 1) * NB, hd * HEAD_DIM:(hd + 1) * HEAD_DIM] = a_buf[pl.ds(t * 8 + hd, NB, stride=16), :].astype(BF16)
    for i in range(4):
        load_o(i).wait()
        part[:, i * QW:(i + 1) * QW] = dot32(att[...], buf_c[i * QW:(i + 1) * QW, QW:2 * QW])

    my_half = pl.ds(pl.multiple_of(c * 64, 64), 64)
    ot_half = pl.ds(pl.multiple_of((1 - c) * 64, 64), 64)
    mine = pl.ds(pl.multiple_of(c * 64 + x * 32, 32), 32)
    away = pl.ds(pl.multiple_of(c * 64 + (1 - x) * 32, 32), 32)

    def reduce_rows(k):
        a1 = remote(part.at[ot_half], r1, ar_s.at[k, 0], ar_r.at[k, 0], pt)
        a1.start()
        if k == 0:
            load_u.start()
        a1.wait_recv()
        x_half = pl.ds(pl.multiple_of((1 - x) * 32, 32), 32)
        part[away, :] = part[away, :] + r1[x_half, :]
        a2 = remote(part.at[away], r2, ar_s.at[k, 1], ar_r.at[k, 1], xs)
        a2.start()
        m_half = pl.ds(pl.multiple_of(x * 32, 32), 32)
        part[mine, :] = part[mine, :] + r1[m_half, :]
        a2.wait_recv()
        a1.wait_send()
        a2.wait_send()
        return part[mine, :] + r2[...]

    def gather_rows(k, buf):
        a3 = remote(buf.at[mine], buf.at[mine], ar_s.at[k, 2], ar_r.at[k, 2], xs)
        a3.start()
        a4 = remote(buf.at[mine], buf.at[mine], ar_s.at[k, 3], ar_r.at[k, 3], pt)
        a4.start()
        a3.wait_recv()
        a5 = remote(buf.at[away], buf.at[away], ar_s.at[k, 4], ar_r.at[k, 4], pt)
        a5.start()
        a4.wait_recv()
        a5.wait_recv()
        a3.wait_send()
        a4.wait_send()
        a5.wait_send()

    hid2[...] = (hid[mine, :].astype(F32) + reduce_rows(0)).astype(BF16)
    n2[mine, :] = norm_rows(hid2[...], g_mlp[...].astype(F32))
    gather_rows(0, n2)

    load_g.wait()
    load_u.wait()

    def mlp_cols(i, carry):
        cols = pl.ds(pl.multiple_of(i * 256, 256), 256)
        gate = dot32(n2[...], buf_b[:, cols])
        up = dot32(n2[...], buf_c[:, cols])
        mid[:, cols] = (gate * (1.0 / (1.0 + jnp.exp(-gate))) * up).astype(BF16)
        return carry

    lax.fori_loop(0, FF // 256, mlp_cols, 0)
    load_d.wait()

    def down_cols(i, carry):
        cols = pl.ds(pl.multiple_of(i * 256, 256), 256)
        part[:, cols] = dot32(mid[...], buf_a[:, cols])
        return carry

    lax.fori_loop(0, D // 256, down_cols, 0)
    out_buf[mine, :] = (hid2[...].astype(F32) + reduce_rows(1)).astype(BF16)
    gather_rows(1, out_buf)
    st_hid = pltpu.make_async_copy(out_buf, o_hid, st_sem.at[NCH + 1])
    st_hid.start()

    for kind in range(3):
        for tn in range(2):
            for j in range(NCH):
                kv_send(kind, tn, j).wait_send()
    for j in range(NCH):
        store_kv(j).wait()
    st_new.wait()
    st_hid.wait()


def solution(mesh):
    seq_spec = P('replica', 'model', None)
    col_spec = P(None, None, 'model')
    row_spec = P(None, 'model', None)
    gain_spec = P(None, None)
    tok_spec = P('replica', None)
    cache_spec = P(None, 'replica', None, 'model', None)
    in_specs = (seq_spec, P('replica'), tok_spec, gain_spec, col_spec, col_spec, col_spec, row_spec, gain_spec, col_spec, col_spec, row_spec)
    out_specs = (tok_spec, tok_spec, cache_spec, cache_spec)

    def per_device(prompt, lengths, new_tok, norm_attn, w_q, w_k, w_v, w_o, norm_mlp, w_gate, w_up, w_down):
        my_idx = lax.axis_index('model')
        loc_c, loc_s = rotate_tables(my_idx * SEQ_LOC + jnp.arange(SEQ_LOC))
        tab_c = jnp.stack([loc_c, jnp.ones_like(loc_c)])
        tab_s = jnp.stack([loc_s, jnp.zeros_like(loc_s)])
        rot_c, rot_s = rotate_tables(jnp.concatenate([lengths - 1, lengths]))
        vmem = pl.BlockSpec(memory_space=pltpu.VMEM)
        hbm = pl.BlockSpec(memory_space=pl.ANY)
        smem = pl.BlockSpec(memory_space=pltpu.SMEM)
        dma = pltpu.SemaphoreType.DMA
        o_hid, o_kv, o_new = pl.pallas_call(
            kernel,
            out_shape=(jax.ShapeDtypeStruct((2 * NB, D), BF16), jax.ShapeDtypeStruct((2, NB, 256, HEAD_DIM), BF16),
                       jax.ShapeDtypeStruct((2, 2 * NB, HEAD_DIM), BF16)),
            in_specs=[smem] + [vmem] * 7 + [hbm] * 8,
            out_specs=(hbm, hbm, hbm),
            scratch_shapes=[
                pltpu.VMEM((NB * SEQ_LOC, D), BF16),
                pltpu.VMEM((D, FF), BF16),
                pltpu.VMEM((D, FF), BF16),
                pltpu.VMEM((2, NB, 256, HEAD_DIM), BF16),
                pltpu.VMEM((3, 2, NCH, CH, 64, HEAD_DIM), BF16),
                pltpu.VMEM((2 * ROWS, HEAD_DIM), F32),
                pltpu.VMEM((NB * 16, HEAD_DIM), F32),
                pltpu.VMEM((NB * 16, HEAD_DIM), F32),
                pltpu.VMEM((NB * 16, HEAD_DIM), F32),
                pltpu.VMEM((NB * 16, HEAD_DIM), F32),
                pltpu.VMEM((2 * NB, QW), BF16),
                pltpu.VMEM((NB, D), BF16),
                pltpu.VMEM((32, D), BF16),
                pltpu.VMEM((2 * NB, D), BF16),
                pltpu.VMEM((2 * NB, D), BF16),
                pltpu.VMEM((2 * NB, D), F32),
                pltpu.VMEM((NB, D), F32),
                pltpu.VMEM((32, D), F32),
                pltpu.VMEM((2 * NB, D), BF16),
                pltpu.VMEM((2 * NB, FF), BF16),
                pltpu.VMEM((32, D), BF16),
                pltpu.VMEM((2 * NB, D), BF16),
                pltpu.VMEM((2, 2 * NB, HEAD_DIM), BF16),
                dma((NCH,)), dma((2,)), dma((8,)), dma((NCH + 2,)),
                dma, dma, dma((WCH,)), dma((WCH,)), dma((WCH,)), dma((WCH,)),
                dma((WCH,)), dma((WCH,)), dma((WCH,)), dma((WCH,)),
                dma((3,)), dma((3,)), dma((3, 2, NCH)), dma((3, 2, NCH)), dma((2, 5)), dma((2, 5)),
            ],
            compiler_params=pltpu.CompilerParams(collective_id=0, has_side_effects=True, vmem_limit_bytes=67043328),
            name="layer",
        )(lengths, tab_c, tab_s, rot_c, rot_s, norm_attn, norm_mlp, new_tok,
          prompt.reshape(NB * SEQ_LOC, D), w_q[0], w_k[0], w_v[0], w_o[0], w_gate[0], w_up[0], w_down[0])
        caches = [jnp.concatenate([o_kv[i].reshape(NB, 128, 2, HEAD_DIM), o_new[i].reshape(NB, 1, 2, HEAD_DIM)], axis=1)[None]
                  for i in range(2)]
        return o_hid[NB:], o_hid[:NB], caches[0], caches[1]

    return jax.shard_map(per_device, mesh=mesh, in_specs=in_specs, out_specs=out_specs, check_vma=False)
```

profile of v0, /device:TPU:0, one launch (start us, length us, event | category | flops | bytes accessed | tf_op | source)
XLA Modules:
  0.0 224.7 jit_solution(1366040985481222037)
XLA Ops:
  0.7 0.7 broadcast_add_fusion
  1.3 0.7 add_convert_fusion
  2.1 0.1 fusion.1
  2.2 0.1 maximum_bitcast_fusion.2
  2.3 0.6 stack.13.tab_c
  2.9 0.6 stack.15.tab_s
  3.5 0.3 fusion
  3.8 0.8 pad_maximum_fusion
  4.6 194.9 %layer.1 = (bf16[128,3072]{1,0:T(8,128)(2,1)}, bf16[2,64,256,128]{3,2,1,0:T(8,128)(2,1)}, bf16[2,128,128]{2,1,0:T(8,128)(2,1)}) custom-call(s32[64]{0:T(128)} %lens.1, f32[2,32,128]{2,1,0:T(8,128)} %stack.13.tab_c, f32[2,32,128]{2,1,0:T(8,128)} %stack.15.tab_s, f32[128,128]{1,0:T(8,128)} %get-tuple-element.24.rot_c, f32[128,128]{1,0:T(8,128)} %get-tuple-element.25.rot_s, ...), custom_call_target="tpu_custom_call" | custom-call | tf_op jit(solution)/shard_map/layer/pallas_call | solution.py:420
  199.5 2.0 fusion.3
  201.6 0.8 fusion.4
  202.4 5.2 %fusion.2 = (bf16[1,64,256,128]{3,2,1,0:T(8,128)(2,1)}, bf16[1,64,256,128]{3,2,1,0:T(8,128)(2,1)S(1)}) fusion(bf16[2,64,256,128]{3,2,1,0:T(8,128)(2,1)} %get-tuple-element.8), kind=kLoop, calls=%fused_computation.16 | loop fusion | bytes 16777216 | tf_op jit(solution)/shard_map/slice | solution.py:459
  207.5 9.7 %maximum_bitcast_fusion.1 = bf16[1,64,129,2,128]{4,3,2,1,0:T(2,128)(2,1)} fusion(bf16[64,1,2,128]{3,2,1,0:T(2,128)(2,1)S(1)} %bitcast.35, bf16[64,128,2,128]{3,2,1,0:T(2,128)(2,1)} %bitcast.25), kind=kLoop, calls=%fused_computation.1 | loop fusion | flops 2113536 | bytes 8454144 | tf_op jit(solution)/shard_map/broadcast_in_dim | solution.py:459
  217.2 7.5 %maximum_bitcast_fusion = bf16[1,64,129,2,128]{4,3,2,1,0:T(2,128)(2,1)} fusion(bf16[64,1,2,128]{3,2,1,0:T(2,128)(2,1)S(1)} %bitcast.34, bf16[64,128,2,128]{3,2,1,0:T(2,128)(2,1)S(1)} %bitcast.24), kind=kLoop, calls=%fused_computation | loop fusion | flops 2113536 | bytes 8454144 | tf_op jit(solution)/shard_map/broadcast_in_dim | solution.py:459
  (2 shorter events, 0.0 us)
where the time goes:
time: 225 us
  Pallas kernels  195 us (87%)
  other arithmetic  19.8 us (9%)
  local copies, waits for them, and re-layouts  9.22 us (4%)
    pallas_call x1, Pallas kernels, per_device(): pl.pallas_call(kernel, out_shape=(jax.ShapeDtypeStruct((2 * NB, D), BF16)...  195 us
    broadcast_in_dim x2, other arithmetic, per_device(): jnp.concatenate([o_kv[i].reshape(NB, 128, 2, HEAD_DIM), o_new[i].reshape(...  17.1 us
    slice x1, local copies, waits for them, and re-layouts, per_device(): o_kv[i].reshape(NB, 128, 2, HEAD_DIM)  5.16 us

commit v1 on v0

--- a/solution.py
+++ b/solution.py
@@ -2,6 +2,7 @@
 
 import jax
 import jax.numpy as jnp
+import numpy as np
 from jax import lax
 from jax.experimental import pallas as pl
 from jax.experimental.pallas import tpu as pltpu
@@ -29,19 +30,19 @@
     return jnp.dot(lhs, rhs, preferred_element_type=F32)
 
 
-def rotate_tables(positions):
+def rotate_tables(n):
     half = HEAD_DIM // 2
-    inv_freq = 10000.0 ** (-2.0 * jnp.arange(half, dtype=F32) / HEAD_DIM)
-    angles = positions.astype(F32)[:, None] * inv_freq
-    cos_tab, sin_tab = jnp.cos(angles), jnp.sin(angles)
-    return jnp.concatenate([cos_tab, cos_tab], 1), jnp.concatenate([-sin_tab, sin_tab], 1)
-
-
-def kernel(lens, tab_c, tab_s, rot_c, rot_s, g_attn, g_mlp, new_tok,
-           prompt, w_q, w_k, w_v, w_o, w_g, w_u, w_d,
-           o_hid, o_kv, o_new,
+    inv_freq = np.float32(10000.0) ** (np.float32(-2.0) * np.arange(half, dtype=np.float32) / np.float32(HEAD_DIM))
+    angles = (np.arange(n, dtype=np.float32)[:, None] * inv_freq).astype(np.float32).astype(np.float64)
+    cos_tab, sin_tab = np.cos(angles), np.sin(angles)
+    return np.stack([np.concatenate([cos_tab, cos_tab], 1), np.concatenate([-sin_tab, sin_tab], 1)]).astype(np.float32)
+
+
+def kernel(lens, tab, g_attn, g_mlp,
+           new_tok, prompt, w_q, w_k, w_v, w_o, w_g, w_u, w_d,
+           o_hid, o_kv,
            buf_a, buf_b, buf_c, kv, stage, flat, q_buf, k_buf, v_buf, a_buf, att,
-           sel_r1, sel_r2, hid, normed, part, r1, r2, n2, mid, hid2, out_buf, knv,
+           sel_r1, sel_r2, hid, normed, part, r1, r2, n2, mid, hid2, out_buf, knv, rot, o_buf,
            ld_p, ld_w, ld_big, st_sem,
            wp_s, wp_r, wx_s, wx_r, wfx_s, wfx_r, wy_s, wy_r, wfy_s, wfy_r,
            sel_s, sel_r, kv_s, kv_r, ar_s, ar_r):
@@ -72,6 +73,8 @@
         load_p(j).start()
     load_q = pltpu.make_async_copy(w_q, buf_c.at[:, pl.ds(0, QW)], ld_big.at[0])
     load_q.start()
+    load_t = pltpu.make_async_copy(new_tok, hid.at[pl.ds(NB, NB)], ld_big.at[8])
+    load_t.start()
 
     def load_o(i):
         return pltpu.make_async_copy(w_o.at[:, pl.ds(i * QW, QW)], buf_c.at[pl.ds(i * QW, QW), pl.ds(QW, QW)], ld_big.at[1 + i])
@@ -152,7 +155,9 @@
     def unit_chunk(owner, h, j):
         col = pl.ds(pl.multiple_of(owner * 512 + h * 256, 256), 256)
         acc = dot32(buf_a[pl.ds(pl.multiple_of(j * ROWS, ROWS), ROWS), :], buf_b[:, col])
-        ct, st = tab_c[h], tab_s[h]
+        here = pl.ds(pl.multiple_of(m * SEQ_LOC, SEQ_LOC), SEQ_LOC)
+        ct = jnp.where(h == 0, tab[0, here, :], 1.0)
+        st = jnp.where(h == 0, tab[1, here, :], 0.0)
         for hd in range(2):
             a = acc[:, hd * HEAD_DIM:(hd + 1) * HEAD_DIM]
             turned = pltpu.roll(a, HEAD_DIM // 2, 1)
@@ -214,7 +219,6 @@
     hid[half, :] = (normed[half, :].astype(F32) + sel_r2[...].astype(F32)).astype(BF16)
     s3 = remote(hid.at[half], hid.at[half], sel_s.at[2], sel_r.at[2], pt)
     s3.start()
-    hid[pl.ds(NB, NB), :] = new_tok[...]
     forward_y(3)
     for r in range(WCH):
         wfy(r).wait_recv()
@@ -226,6 +230,7 @@
 
     lax.fori_loop(0, NCH, last_units, 0)
     s3.wait()
+    load_t.wait()
 
     def norm_rows(src, gain):
         v = src.astype(F32)
@@ -243,6 +248,15 @@
     k_buf[...] = jnp.zeros_like(k_buf)
     v_buf[...] = jnp.zeros_like(v_buf)
 
+    def pick(b, carry):
+        pos = jnp.clip(lens[b], 1, 128)
+        for i in range(2):
+            rot[i, pl.ds(b, 1), :] = tab[i, pl.ds(pos - 1, 1), :]
+            rot[i, pl.ds(NB + b, 1), :] = tab[i, pl.ds(pos, 1), :]
+        return carry
+
+    lax.fori_loop(0, NB, pick, 0)
+
     def turn(a, ct, st):
         return (a * ct + pltpu.roll(a, HEAD_DIM // 2, 1) * st).astype(BF16).astype(F32)
 
@@ -250,15 +264,15 @@
         qs = dot32(normed[...], buf_c[:, pair * 256:(pair + 1) * 256])
         for i in range(2):
             hd = pair * 2 + i
-            rot = turn(qs[:, i * HEAD_DIM:(i + 1) * HEAD_DIM], rot_c[...], rot_s[...])
+            q_h = turn(qs[:, i * HEAD_DIM:(i + 1) * HEAD_DIM], rot[0], rot[1])
             for t in range(2):
-                q_buf[pl.ds(t * 8 + hd, NB, stride=16), :] = rot[t * NB:(t + 1) * NB]
+                q_buf[pl.ds(t * 8 + hd, NB, stride=16), :] = q_h[t * NB:(t + 1) * NB]
     toks = normed[NB:2 * NB, :]
     k_new = dot32(toks, buf_b[:, pl.ds(pl.multiple_of(m * 512, 256), 256)])
     v_new = dot32(toks, buf_b[:, pl.ds(pl.multiple_of(m * 512 + 256, 256), 256)])
     for g in range(2):
         cols = slice(g * HEAD_DIM, (g + 1) * HEAD_DIM)
-        k_g = turn(k_new[:, cols], rot_c[NB:, :], rot_s[NB:, :])
+        k_g = turn(k_new[:, cols], rot[0, NB:, :], rot[1, NB:, :])
         v_g = v_new[:, cols].astype(BF16).astype(F32)
         flat[pl.ds(g, NB, stride=2), :] = k_g
         flat[pl.ds(2 * NB + g, NB, stride=2), :] = v_g
@@ -268,8 +282,6 @@
             v_buf[rows, :] = v_g
     knv[0] = flat[0:2 * NB, :].astype(BF16)
     knv[1] = flat[2 * NB:4 * NB, :].astype(BF16)
-    st_new = pltpu.make_async_copy(knv, o_new, st_sem.at[NCH])
-    st_new.start()
 
     wp.wait_send()
     for r in range(WCH):
@@ -305,16 +317,31 @@
             attend(i * 4 + t)
         return carry
 
-    def store_kv(j):
-        r = pl.ds(j * CH, CH)
-        return pltpu.make_async_copy(kv.at[:, r], o_kv.at[:, r], st_sem.at[j])
+    def store_kv(h, g):
+        rows = pl.ds(pl.multiple_of(g * 2064, 2064), 2064)
+        return pltpu.make_async_copy(o_buf.at[h, pl.ds(0, 2064)], o_kv.at[h, rows], st_sem.at[h])
+
+    def lay_out(g, carry):
+        @pl.when(g > 0)
+        def _():
+            for h in range(2):
+                store_kv(h, g - 1).wait()
+        for h in range(2):
+            for t in range(8):
+                o_buf[h, t * 258:t * 258 + 256, :] = kv[h, g * 8 + t]
+            new = knv[h, pl.ds(pl.multiple_of(g * 16, 16), 16), :]
+            for t in range(8):
+                o_buf[h, t * 258 + 256:t * 258 + 258, :] = new[2 * t:2 * t + 2]
+            store_kv(h, g).start()
+        return carry
 
     for j in range(NCH):
         for kind in range(3):
             for tn in range(2):
                 kv_send(kind, tn, j).wait_recv()
-        store_kv(j).start()
         lax.fori_loop(j * (CH // 4), (j + 1) * (CH // 4), attend_four, 0)
+        if j < NCH - 1:
+            lax.fori_loop(j * (CH // 8), (j + 1) * (CH // 8), lay_out, 0)
 
     for hd in range(6):
         for t in range(2):
@@ -340,6 +367,8 @@
         a2.start()
         m_half = pl.ds(pl.multiple_of(x * 32, 32), 32)
         part[mine, :] = part[mine, :] + r1[m_half, :]
+        if k == 0:
+            lax.fori_loop((NCH - 1) * (CH // 8), NB // 8, lay_out, 0)
         a2.wait_recv()
         a1.wait_send()
         a2.wait_send()
@@ -384,16 +413,15 @@
     lax.fori_loop(0, D // 256, down_cols, 0)
     out_buf[mine, :] = (hid2[...].astype(F32) + reduce_rows(1)).astype(BF16)
     gather_rows(1, out_buf)
-    st_hid = pltpu.make_async_copy(out_buf, o_hid, st_sem.at[NCH + 1])
+    st_hid = pltpu.make_async_copy(out_buf, o_hid, st_sem.at[2])
     st_hid.start()
 
     for kind in range(3):
         for tn in range(2):
             for j in range(NCH):
                 kv_send(kind, tn, j).wait_send()
-    for j in range(NCH):
-        store_kv(j).wait()
-    st_new.wait()
+    for h in range(2):
+        store_kv(h, NB // 8 - 1).wait()
     st_hid.wait()
 
 
@@ -408,21 +436,16 @@
     out_specs = (tok_spec, tok_spec, cache_spec, cache_spec)
 
     def per_device(prompt, lengths, new_tok, norm_attn, w_q, w_k, w_v, w_o, norm_mlp, w_gate, w_up, w_down):
-        my_idx = lax.axis_index('model')
-        loc_c, loc_s = rotate_tables(my_idx * SEQ_LOC + jnp.arange(SEQ_LOC))
-        tab_c = jnp.stack([loc_c, jnp.ones_like(loc_c)])
-        tab_s = jnp.stack([loc_s, jnp.zeros_like(loc_s)])
-        rot_c, rot_s = rotate_tables(jnp.concatenate([lengths - 1, lengths]))
+        tab = jnp.asarray(rotate_tables(136))
         vmem = pl.BlockSpec(memory_space=pltpu.VMEM)
         hbm = pl.BlockSpec(memory_space=pl.ANY)
         smem = pl.BlockSpec(memory_space=pltpu.SMEM)
         dma = pltpu.SemaphoreType.DMA
-        o_hid, o_kv, o_new = pl.pallas_call(
+        o_hid, o_kv = pl.pallas_call(
             kernel,
-            out_shape=(jax.ShapeDtypeStruct((2 * NB, D), BF16), jax.ShapeDtypeStruct((2, NB, 256, HEAD_DIM), BF16),
-                       jax.ShapeDtypeStruct((2, 2 * NB, HEAD_DIM), BF16)),
-            in_specs=[smem] + [vmem] * 7 + [hbm] * 8,
-            out_specs=(hbm, hbm, hbm),
+            out_shape=(jax.ShapeDtypeStruct((2 * NB, D), BF16), jax.ShapeDtypeStruct((2, NB * 258, HEAD_DIM), BF16)),
+            in_specs=[smem] + [vmem] * 3 + [hbm] * 9,
+            out_specs=(hbm, hbm),
             scratch_shapes=[
                 pltpu.VMEM((NB * SEQ_LOC, D), BF16),
                 pltpu.VMEM((D, FF), BF16),
@@ -447,17 +470,18 @@
                 pltpu.VMEM((32, D), BF16),
                 pltpu.VMEM((2 * NB, D), BF16),
                 pltpu.VMEM((2, 2 * NB, HEAD_DIM), BF16),
-                dma((NCH,)), dma((2,)), dma((8,)), dma((NCH + 2,)),
+                pltpu.VMEM((2, 2 * NB, HEAD_DIM), F32),
+                pltpu.VMEM((2, 8 * 258 + 32, HEAD_DIM), BF16),
+                dma((NCH,)), dma((2,)), dma((9,)), dma((3,)),
                 dma, dma, dma((WCH,)), dma((WCH,)), dma((WCH,)), dma((WCH,)),
                 dma((WCH,)), dma((WCH,)), dma((WCH,)), dma((WCH,)),
                 dma((3,)), dma((3,)), dma((3, 2, NCH)), dma((3, 2, NCH)), dma((2, 5)), dma((2, 5)),
             ],
             compiler_params=pltpu.CompilerParams(collective_id=0, has_side_effects=True, vmem_limit_bytes=67043328),
             name="layer",
-        )(lengths, tab_c, tab_s, rot_c, rot_s, norm_attn, norm_mlp, new_tok,
+        )(lengths, tab, norm_attn, norm_mlp, new_tok,
           prompt.reshape(NB * SEQ_LOC, D), w_q[0], w_k[0], w_v[0], w_o[0], w_gate[0], w_up[0], w_down[0])
-        caches = [jnp.concatenate([o_kv[i].reshape(NB, 128, 2, HEAD_DIM), o_new[i].reshape(NB, 1, 2, HEAD_DIM)], axis=1)[None]
-                  for i in range(2)]
+        caches = o_kv.reshape(2, 1, NB, 129, 2, HEAD_DIM)
         return o_hid[NB:], o_hid[:NB], caches[0], caches[1]
 
     return jax.shard_map(per_device, mesh=mesh, in_specs=in_specs, out_specs=out_specs, check_vma=False)

time: 225 us -> 205 us (0.911)
  other arithmetic: 19.8 us -> 0 us
    broadcast_in_dim x2 -> x0, other arithmetic: 17.1 us -> none  [per_device(): jnp.concatenate([o_kv[i].reshape(NB, 128, 2, HEAD_DIM), o_new[i].reshape(...]
    slice x1 -> x2, local copies, waits for them, and re-layouts: 2.04 us -> 9.67 us  [per_device(): return (o_hid[NB:], o_hid[:NB], caches[0], caches[1])]
    slice x2 -> x0, local copies, waits for them, and re-layouts: 5.94 us -> none  [the longest x1 5.16 us: per_device(): o_kv[i].reshape(NB, 128, 2, HEAD_DIM)]
where the time goes in v1:
time: 205 us
  Pallas kernels  195 us (95%)
  local copies, waits for them, and re-layouts  9.67 us (5%)
    pallas_call x1, Pallas kernels, per_device(): pl.pallas_call(kernel, out_shape=(jax.ShapeDtypeStruct((2 * NB, D), BF16)...  195 us
    slice x2, local copies, waits for them, and re-layouts, per_device(): return (o_hid[NB:], o_hid[:NB], caches[0], caches[1])  9.67 us

profile of v1, /device:TPU:0, one launch (start us, length us, event | category | flops | bytes accessed | tf_op | source)
XLA Modules:
  0.0 205.2 jit_solution(13611308090698362560)
XLA Ops:
  0.6 194.9 %layer.1 = (bf16[128,3072]{1,0:T(8,128)(2,1)}, bf16[2,16512,128]{2,1,0:T(8,128)(2,1)}) custom-call(s32[64]{0:T(128)} %lens.1, f32[2,136,128]{2,1,0:T(8,128)} %constant.2.clone.tab, bf16[1,3072]{1,0:T(2,128)(2,1)} %g_attn.1, bf16[1,3072]{1,0:T(2,128)(2,1)} %g_mlp.1, bf16[64,3072]{1,0:T(8,128)(2,1)} %new_tok.1, bf16[2048,3072]{1,0:T(8,128)(2,1)} %bitcast.10, ...), custom_call_target="tpu_custom_call" | custom-call | tf_op jit(solution)/shard_map/layer/pallas_call | solution.py:444
  195.5 2.0 fusion.1
  197.6 7.6 %fusion = (bf16[1,16512,128]{2,1,0:T(8,128)(2,1)}, bf16[1,16512,128]{2,1,0:T(8,128)(2,1)}) fusion(bf16[2,16512,128]{2,1,0:T(8,128)(2,1)} %get-tuple-element.7), kind=kLoop, calls=%fused_computation | loop fusion | bytes 16908288 | tf_op jit(solution)/shard_map/slice | solution.py:485

commit v2 on v1

--- a/solution.py
+++ b/solution.py
@@ -40,9 +40,9 @@
 
 def kernel(lens, tab, g_attn, g_mlp,
            new_tok, prompt, w_q, w_k, w_v, w_o, w_g, w_u, w_d,
-           o_hid, o_kv,
+           o_last, o_dec, o_k, o_v,
            buf_a, buf_b, buf_c, kv, stage, flat, q_buf, k_buf, v_buf, a_buf, att,
-           sel_r1, sel_r2, hid, normed, part, r1, r2, n2, mid, hid2, out_buf, knv, rot, o_buf,
+           sel_r1, sel_r2, hid, normed, part, r1, r2, x2, mid, p_buf, out_buf, knv, rot, o_buf,
            ld_p, ld_w, ld_big, st_sem,
            wp_s, wp_r, wx_s, wx_r, wfx_s, wfx_r, wy_s, wy_r, wfy_s, wfy_r,
            sel_s, sel_r, kv_s, kv_r, ar_s, ar_r):
@@ -90,8 +90,9 @@
         pl.semaphore_signal(barrier, inc=1, device_id=dev, device_id_type=MESH)
     pl.semaphore_wait(barrier, 4)
 
-    def w_ref(owner, h, r):
-        return buf_b.at[pl.ds(r * WROWS, WROWS), pl.ds(pl.multiple_of(owner * 512 + h * 256, 256), 256)]
+    def w_ref(owner, half, r):
+        rows = pl.ds(pl.multiple_of(half * (D // 2) + (r % 2) * WROWS, WROWS), WROWS)
+        return buf_b.at[rows, pl.ds(pl.multiple_of(owner * 512 + (r // 2) * 256, 256), 256)]
 
     def wx(r):
         ref = w_ref(m, y, r)
@@ -156,71 +157,69 @@
         col = pl.ds(pl.multiple_of(owner * 512 + h * 256, 256), 256)
         acc = dot32(buf_a[pl.ds(pl.multiple_of(j * ROWS, ROWS), ROWS), :], buf_b[:, col])
         here = pl.ds(pl.multiple_of(m * SEQ_LOC, SEQ_LOC), SEQ_LOC)
-        ct = jnp.where(h == 0, tab[0, here, :], 1.0)
-        st = jnp.where(h == 0, tab[1, here, :], 0.0)
         for hd in range(2):
             a = acc[:, hd * HEAD_DIM:(hd + 1) * HEAD_DIM]
-            turned = pltpu.roll(a, HEAD_DIM // 2, 1)
-            res = a.reshape(CH, SEQ_LOC, HEAD_DIM) * ct[None] + turned.reshape(CH, SEQ_LOC, HEAD_DIM) * st[None]
-            flat[pl.ds(hd, ROWS, stride=2), :] = res.reshape(ROWS, HEAD_DIM)
+            if h == 0:
+                turned = pltpu.roll(a, HEAD_DIM // 2, 1).reshape(CH, SEQ_LOC, HEAD_DIM)
+                a = a.reshape(CH, SEQ_LOC, HEAD_DIM) * tab[0, here, :][None] + turned * tab[1, here, :][None]
+                a = a.reshape(ROWS, HEAD_DIM)
+            flat[pl.ds(hd, ROWS, stride=2), :] = a
         return flat[...].astype(BF16).reshape(CH, 2 * SEQ_LOC, HEAD_DIM)
 
     def kv_ref(h, j):
         return kv.at[h, pl.ds(pl.multiple_of(j * CH, CH), CH), pl.ds(pl.multiple_of(m * 64, 64), 64)]
 
-    def kv_send(kind, turn, j):
+    def kv_send(kind, h, j):
         dev = (pt, xs, xo)[kind]
-        h = y if turn == 0 else 1 - y
-        return remote(stage.at[kind, turn, j], kv_ref(h, j), kv_s.at[kind, turn, j], kv_r.at[kind, turn, j], dev)
-
-    def run_unit(kind, turn, j):
+        return remote(stage.at[kind, h, j], kv_ref(h, j), kv_s.at[kind, h, j], kv_r.at[kind, h, j], dev)
+
+    def run_unit(kind, h, j):
         owner = (pt_m, xs_m, xo_m)[kind]
-        h = y if turn == 0 else 1 - y
-        stage[kind, turn, j] = unit_chunk(owner, h, j)
-        kv_send(kind, turn, j).start()
+        stage[kind, h, j] = unit_chunk(owner, h, j)
+        kv_send(kind, h, j).start()
+
+    def own_unit(h):
+        def body(j, carry):
+            kv[h, pl.ds(pl.multiple_of(j * CH, CH), CH), pl.ds(pl.multiple_of(m * 64, 64), 64)] = unit_chunk(m, h, j)
+            return carry
+        lax.fori_loop(0, NCH, body, 0)
+
+    def loop_unit(kind, h):
+        def body(j, carry):
+            run_unit(kind, h, j)
+            return carry
+        lax.fori_loop(0, NCH, body, 0)
 
     forward_x(0)
-
-    def own_units(i, carry):
-        h, j = i // NCH, lax.rem(i, NCH)
-        kv[h, pl.ds(pl.multiple_of(j * CH, CH), CH), pl.ds(pl.multiple_of(m * 64, 64), 64)] = unit_chunk(m, h, j)
-        return carry
-
-    lax.fori_loop(0, 2 * NCH, own_units, 0)
-    forward_x(1)
-
+    own_unit(0)
     s1.wait()
     sel_b[...] = (sel_b[...].astype(F32) + sel_r1[...].astype(F32)).astype(BF16)
     half = pl.ds(pl.multiple_of(c * 32, 32), 32)
     s2 = remote(normed.at[half], sel_r2, sel_s.at[1], sel_r.at[1], xs)
     s2.start()
-
+    own_unit(1)
+    forward_x(1)
+    forward_y(0)
     wp.wait_recv()
-
-    def loop_unit(kind, turn):
-        def body(j, carry):
-            run_unit(kind, turn, j)
-            return carry
-        lax.fori_loop(0, NCH, body, 0)
-
     loop_unit(0, 0)
     forward_x(2)
-    forward_y(0)
+    forward_y(1)
+    loop_unit(1, 0)
+    for r in range(2):
+        wfx(r).wait_recv()
+        wfy(r).wait_recv()
+    loop_unit(2, 0)
+    forward_x(3)
+    forward_y(2)
     loop_unit(0, 1)
-    forward_x(3)
-    loop_unit(1, 0)
-    forward_y(1)
-    for r in range(WCH):
-        wfx(r).wait_recv()
-    loop_unit(2, 0)
-    forward_y(2)
 
     s2.wait()
     hid[half, :] = (normed[half, :].astype(F32) + sel_r2[...].astype(F32)).astype(BF16)
     s3 = remote(hid.at[half], hid.at[half], sel_s.at[2], sel_r.at[2], pt)
     s3.start()
     forward_y(3)
-    for r in range(WCH):
+    for r in range(2, WCH):
+        wfx(r).wait_recv()
         wfy(r).wait_recv()
 
     def last_units(j, carry):
@@ -299,7 +298,7 @@
     is_new = lax.broadcasted_iota(jnp.int32, (16, 1), 0) >= 8
     scale = HEAD_DIM ** -0.5
 
-    def attend(b):
+    def score(b):
         rows = pl.ds(pl.multiple_of(b * 16, 16), 16)
         q = q_buf[rows, :]
         s = lax.dot_general(q.astype(BF16), kv[0, b], (((1,), (1,)), ((), ())), preferred_element_type=F32) * scale
@@ -308,113 +307,143 @@
         top = jnp.maximum(jnp.max(s, axis=-1, keepdims=True), s_new)
         p = jnp.exp(s - top)
         p_new = jnp.exp(s_new - top)
-        total = jnp.sum(p, axis=-1, keepdims=True) + p_new
-        acc = dot32(p.astype(BF16), kv[1, b]) + p_new * v_buf[rows, :]
-        a_buf[rows, :] = acc / total
-
-    def attend_four(i, carry):
+        inv = 1.0 / (jnp.sum(p, axis=-1, keepdims=True) + p_new)
+        p_buf[rows, :] = (p * inv).astype(BF16)
+        a_buf[rows, :] = (p_new * inv) * v_buf[rows, :]
+
+    def score_four(i, carry):
         for t in range(4):
-            attend(i * 4 + t)
+            score(i * 4 + t)
+        return carry
+
+    def weigh_eight(i, carry):
+        for t in range(8):
+            b = i * 8 + t
+            rows = pl.ds(pl.multiple_of(b * 16, 16), 16)
+            a_buf[rows, :] = a_buf[rows, :] + dot32(p_buf[rows, :], kv[1, b])
         return carry
 
     def store_kv(h, g):
         rows = pl.ds(pl.multiple_of(g * 2064, 2064), 2064)
-        return pltpu.make_async_copy(o_buf.at[h, pl.ds(0, 2064)], o_kv.at[h, rows], st_sem.at[h])
-
-    def lay_out(g, carry):
-        @pl.when(g > 0)
-        def _():
-            for h in range(2):
+        return pltpu.make_async_copy(o_buf.at[h, pl.ds(0, 2064)], (o_k, o_v)[h].at[rows], st_sem.at[h])
+
+    def lay_out(h):
+        def body(g, carry):
+            @pl.when(g > 0)
+            def _():
                 store_kv(h, g - 1).wait()
-        for h in range(2):
             for t in range(8):
                 o_buf[h, t * 258:t * 258 + 256, :] = kv[h, g * 8 + t]
             new = knv[h, pl.ds(pl.multiple_of(g * 16, 16), 16), :]
             for t in range(8):
                 o_buf[h, t * 258 + 256:t * 258 + 258, :] = new[2 * t:2 * t + 2]
             store_kv(h, g).start()
-        return carry
+            return carry
+        return body
 
     for j in range(NCH):
         for kind in range(3):
-            for tn in range(2):
-                kv_send(kind, tn, j).wait_recv()
-        lax.fori_loop(j * (CH // 4), (j + 1) * (CH // 4), attend_four, 0)
+            kv_send(kind, 0, j).wait_recv()
+        lax.fori_loop(j * (CH // 4), (j + 1) * (CH // 4), score_four, 0)
+        lax.fori_loop(j * (CH // 8), (j + 1) * (CH // 8), lay_out(0), 0)
+    for j in range(NCH):
+        for kind in range(3):
+            kv_send(kind, 1, j).wait_recv()
+        lax.fori_loop(j * (CH // 8), (j + 1) * (CH // 8), weigh_eight, 0)
         if j < NCH - 1:
-            lax.fori_loop(j * (CH // 8), (j + 1) * (CH // 8), lay_out, 0)
+            lax.fori_loop(j * (CH // 8), (j + 1) * (CH // 8), lay_out(1), 0)
 
     for hd in range(6):
         for t in range(2):
             att[t * NB:(t + 1) * NB, hd * HEAD_DIM:(hd + 1) * HEAD_DIM] = a_buf[pl.ds(t * 8 + hd, NB, stride=16), :].astype(BF16)
-    for i in range(4):
-        load_o(i).wait()
-        part[:, i * QW:(i + 1) * QW] = dot32(att[...], buf_c[i * QW:(i + 1) * QW, QW:2 * QW])
-
-    my_half = pl.ds(pl.multiple_of(c * 64, 64), 64)
     ot_half = pl.ds(pl.multiple_of((1 - c) * 64, 64), 64)
     mine = pl.ds(pl.multiple_of(c * 64 + x * 32, 32), 32)
     away = pl.ds(pl.multiple_of(c * 64 + (1 - x) * 32, 32), 32)
-
-    def reduce_rows(k):
-        a1 = remote(part.at[ot_half], r1, ar_s.at[k, 0], ar_r.at[k, 0], pt)
-        a1.start()
-        if k == 0:
-            load_u.start()
-        a1.wait_recv()
-        x_half = pl.ds(pl.multiple_of((1 - x) * 32, 32), 32)
-        part[away, :] = part[away, :] + r1[x_half, :]
-        a2 = remote(part.at[away], r2, ar_s.at[k, 1], ar_r.at[k, 1], xs)
-        a2.start()
-        m_half = pl.ds(pl.multiple_of(x * 32, 32), 32)
-        part[mine, :] = part[mine, :] + r1[m_half, :]
-        if k == 0:
-            lax.fori_loop((NCH - 1) * (CH // 8), NB // 8, lay_out, 0)
-        a2.wait_recv()
-        a1.wait_send()
-        a2.wait_send()
-        return part[mine, :] + r2[...]
-
-    def gather_rows(k, buf):
-        a3 = remote(buf.at[mine], buf.at[mine], ar_s.at[k, 2], ar_r.at[k, 2], xs)
-        a3.start()
-        a4 = remote(buf.at[mine], buf.at[mine], ar_s.at[k, 3], ar_r.at[k, 3], pt)
-        a4.start()
-        a3.wait_recv()
-        a5 = remote(buf.at[away], buf.at[away], ar_s.at[k, 4], ar_r.at[k, 4], pt)
-        a5.start()
-        a4.wait_recv()
-        a5.wait_recv()
-        a3.wait_send()
-        a4.wait_send()
-        a5.wait_send()
-
-    hid2[...] = (hid[mine, :].astype(F32) + reduce_rows(0)).astype(BF16)
-    n2[mine, :] = norm_rows(hid2[...], g_mlp[...].astype(F32))
-    gather_rows(0, n2)
-
+    mine_r1 = pl.ds(pl.multiple_of(x * 32, 32), 32)
+    away_r1 = pl.ds(pl.multiple_of((1 - x) * 32, 32), 32)
+
+    def reduce_all(k, produce, after, resid, buf):
+        def msg(step, i, src, dst, dev):
+            return remote(src, dst, ar_s.at[k, step, i], ar_r.at[k, step, i], dev)
+
+        cols = [pl.ds(i * QW, QW) for i in range(4)]
+        a1 = [msg(0, i, part.at[ot_half, cols[i]], r1.at[:, cols[i]], pt) for i in range(4)]
+        a2 = [msg(1, i, part.at[away, cols[i]], r2.at[:, cols[i]], xs) for i in range(4)]
+        a3 = [msg(2, i, buf.at[mine, cols[i]], buf.at[mine, cols[i]], xs) for i in range(4)]
+        a4 = [msg(3, i, buf.at[mine, cols[i]], buf.at[mine, cols[i]], pt) for i in range(4)]
+        a5 = [msg(4, i, buf.at[away, cols[i]], buf.at[away, cols[i]], pt) for i in range(4)]
+
+        def over_x(i):
+            a1[i].wait_recv()
+            part[away, cols[i]] = part[away, cols[i]] + r1[away_r1, cols[i]]
+            a2[i].start()
+            part[mine, cols[i]] = part[mine, cols[i]] + r1[mine_r1, cols[i]]
+
+        for i in range(4):
+            produce(i)
+            a1[i].start()
+            if i:
+                over_x(i - 1)
+        over_x(3)
+        after()
+        for i in range(4):
+            a2[i].wait_recv()
+            total = part[mine, cols[i]] + r2[:, cols[i]]
+            buf[mine, cols[i]] = (resid[mine, cols[i]].astype(F32) + total).astype(BF16)
+            a3[i].start()
+            a4[i].start()
+        for i in range(4):
+            a3[i].wait_recv()
+            a5[i].start()
+        for i in range(4):
+            a4[i].wait_recv()
+            a5[i].wait_recv()
+        for step in (a1, a2, a3, a4, a5):
+            for i in range(4):
+                step[i].wait_send()
+
+    def w_o_cols(i):
+        load_o(i).wait()
+        part[:, i * QW:(i + 1) * QW] = dot32(att[...], buf_c[i * QW:(i + 1) * QW, QW:2 * QW])
+
+    def after_w_o():
+        load_u.start()
+        lax.fori_loop((NCH - 1) * (CH // 8), NB // 8, lay_out(1), 0)
+
+    reduce_all(0, w_o_cols, after_w_o, hid, x2)
+    gain_m = g_mlp[...].astype(F32)
+
+    def norm_x2(i, carry):
+        rows = pl.ds(pl.multiple_of(i * 32, 32), 32)
+        normed[rows, :] = norm_rows(x2[rows, :], gain_m)
+        return carry
+
+    lax.fori_loop(0, 4, norm_x2, 0)
     load_g.wait()
     load_u.wait()
 
     def mlp_cols(i, carry):
         cols = pl.ds(pl.multiple_of(i * 256, 256), 256)
-        gate = dot32(n2[...], buf_b[:, cols])
-        up = dot32(n2[...], buf_c[:, cols])
+        gate = dot32(normed[...], buf_b[:, cols])
+        up = dot32(normed[...], buf_c[:, cols])
         mid[:, cols] = (gate * (1.0 / (1.0 + jnp.exp(-gate))) * up).astype(BF16)
         return carry
 
     lax.fori_loop(0, FF // 256, mlp_cols, 0)
     load_d.wait()
 
-    def down_cols(i, carry):
-        cols = pl.ds(pl.multiple_of(i * 256, 256), 256)
-        part[:, cols] = dot32(mid[...], buf_a[:, cols])
-        return carry
-
-    lax.fori_loop(0, D // 256, down_cols, 0)
-    out_buf[mine, :] = (hid2[...].astype(F32) + reduce_rows(1)).astype(BF16)
-    gather_rows(1, out_buf)
-    st_hid = pltpu.make_async_copy(out_buf, o_hid, st_sem.at[2])
-    st_hid.start()
+    def down_cols(i):
+        def body(t, carry):
+            cols = pl.ds(pl.multiple_of(i * QW + t * 256, 256), 256)
+            part[:, cols] = dot32(mid[...], buf_a[:, cols])
+            return carry
+        lax.fori_loop(0, QW // 256, body, 0)
+
+    reduce_all(1, down_cols, lambda: None, x2, out_buf)
+    st_last = pltpu.make_async_copy(out_buf.at[pl.ds(0, NB)], o_last, st_sem.at[2])
+    st_dec = pltpu.make_async_copy(out_buf.at[pl.ds(NB, NB)], o_dec, st_sem.at[3])
+    st_last.start()
+    st_dec.start()
 
     for kind in range(3):
         for tn in range(2):
@@ -422,7 +451,8 @@
                 kv_send(kind, tn, j).wait_send()
     for h in range(2):
         store_kv(h, NB // 8 - 1).wait()
-    st_hid.wait()
+    st_last.wait()
+    st_dec.wait()
 
 
 def solution(mesh):
@@ -441,11 +471,11 @@
         hbm = pl.BlockSpec(memory_space=pl.ANY)
         smem = pl.BlockSpec(memory_space=pltpu.SMEM)
         dma = pltpu.SemaphoreType.DMA
-        o_hid, o_kv = pl.pallas_call(
+        o_last, o_dec, o_k, o_v = pl.pallas_call(
             kernel,
-            out_shape=(jax.ShapeDtypeStruct((2 * NB, D), BF16), jax.ShapeDtypeStruct((2, NB * 258, HEAD_DIM), BF16)),
+            out_shape=(jax.ShapeDtypeStruct((NB, D), BF16),) * 2 + (jax.ShapeDtypeStruct((NB * 258, HEAD_DIM), BF16),) * 2,
             in_specs=[smem] + [vmem] * 3 + [hbm] * 9,
-            out_specs=(hbm, hbm),
+            out_specs=(hbm,) * 4,
             scratch_shapes=[
                 pltpu.VMEM((NB * SEQ_LOC, D), BF16),
                 pltpu.VMEM((D, FF), BF16),
@@ -467,21 +497,21 @@
                 pltpu.VMEM((32, D), F32),
                 pltpu.VMEM((2 * NB, D), BF16),
                 pltpu.VMEM((2 * NB, FF), BF16),
-                pltpu.VMEM((32, D), BF16),
+                pltpu.VMEM((NB * 16, 256), BF16),
                 pltpu.VMEM((2 * NB, D), BF16),
                 pltpu.VMEM((2, 2 * NB, HEAD_DIM), BF16),
                 pltpu.VMEM((2, 2 * NB, HEAD_DIM), F32),
                 pltpu.VMEM((2, 8 * 258 + 32, HEAD_DIM), BF16),
-                dma((NCH,)), dma((2,)), dma((9,)), dma((3,)),
+                dma((NCH,)), dma((2,)), dma((9,)), dma((4,)),
                 dma, dma, dma((WCH,)), dma((WCH,)), dma((WCH,)), dma((WCH,)),
                 dma((WCH,)), dma((WCH,)), dma((WCH,)), dma((WCH,)),
-                dma((3,)), dma((3,)), dma((3, 2, NCH)), dma((3, 2, NCH)), dma((2, 5)), dma((2, 5)),
+                dma((3,)), dma((3,)), dma((3, 2, NCH)), dma((3, 2, NCH)), dma((2, 5, 4)), dma((2, 5, 4)),
             ],
             compiler_params=pltpu.CompilerParams(collective_id=0, has_side_effects=True, vmem_limit_bytes=67043328),
             name="layer",
         )(lengths, tab, norm_attn, norm_mlp, new_tok,
           prompt.reshape(NB * SEQ_LOC, D), w_q[0], w_k[0], w_v[0], w_o[0], w_gate[0], w_up[0], w_down[0])
-        caches = o_kv.reshape(2, 1, NB, 129, 2, HEAD_DIM)
-        return o_hid[NB:], o_hid[:NB], caches[0], caches[1]
+        caches = [o.reshape(1, NB, 129, 2, HEAD_DIM) for o in (o_k, o_v)]
+        return o_dec, o_last, caches[0], caches[1]
 
     return jax.shard_map(per_device, mesh=mesh, in_specs=in_specs, out_specs=out_specs, check_vma=False)

time: 205 us -> 197 us (0.961)
  Pallas kernels: 195 us -> 183 us
  local copies, waits for them, and re-layouts: 9.67 us -> 12.8 us
    unnamed x0 -> x8, local copies, waits for them, and re-layouts: none -> 12.8 us
    pallas_call x1, Pallas kernels: 195 us -> 183 us  [per_device(): pl.pallas_call(kernel, out_shape=(jax.ShapeDtypeStruct((NB, D), BF16),) *...]
    slice x2 -> x0, local copies, waits for them, and re-layouts: 9.67 us -> none  [per_device(): return (o_hid[NB:], o_hid[:NB], caches[0], caches[1])]
where the time goes in v2:
time: 197 us
  Pallas kernels  183 us (93%)
  local copies, waits for them, and re-layouts  12.8 us (6%)
    pallas_call x1, Pallas kernels, per_device(): pl.pallas_call(kernel, out_shape=(jax.ShapeDtypeStruct((NB, D), BF16),) *...  183 us
    unnamed x8, local copies, waits for them, and re-layouts  12.8 us

profile of v2, /device:TPU:0, one launch (start us, length us, event | category | flops | bytes accessed | tf_op | source)
XLA Modules:
  0.0 196.5 jit_solution(4421860929090506089)
XLA Ops:
  0.6 183.0 %layer.1 = (bf16[64,3072]{1,0:T(8,128)(2,1)}, bf16[64,3072]{1,0:T(8,128)(2,1)}, bf16[16512,128]{1,0:T(8,128)(2,1)}, bf16[16512,128]{1,0:T(8,128)(2,1)}) custom-call(s32[64]{0:T(128)} %lens.1, f32[2,136,128]{2,1,0:T(8,128)} %constant.2.clone.tab, bf16[1,3072]{1,0:T(2,128)(2,1)} %g_attn.1, bf16[1,3072]{1,0:T(2,128)(2,1)} %g_mlp.1, bf16[64,3072]{1,0:T(8,128)(2,1)} %new_tok.1, ...), custom_call_target="tpu_custom_call" | custom-call | tf_op jit(solution)/shard_map/layer/pallas_call | solution.py:474
  183.7 1.8 copy.21
  185.4 0.0 slice-start
  185.4 1.9 copy.22
  187.3 0.0 slice-start.1
  187.3 7.1 %copy.23 = bf16[1,64,129,2,128]{4,3,2,1,0:T(2,128)(2,1)} copy(bf16[1,64,129,2,128]{4,3,2,1,0:T(2,128)(2,1)} %bitcast.19) | data formatting | bytes 8454144
  194.5 0.0 slice-done
  194.5 0.0 slice-done.1
  194.5 2.0 %copy.24 = bf16[1,64,129,2,128]{4,3,2,1,0:T(2,128)(2,1)} copy(bf16[1,64,129,2,128]{4,3,2,1,0:T(2,128)(2,1)S(1)} %bitcast.18) | data formatting | bytes 8454144
  (1 shorter events, 0.0 us)
Async XLA Ops:
  185.4 9.0 %slice-start = ((s8[4227072]{0:T(1024)(128)(4,1)}), s8[4194304]{0:T(1024)(128)(4,1)S(1)}, s32[]{:S(2)}) async-start(s8[4227072]{0:T(1024)(128)(4,1)} %bitcast.16), calls=%async_computation | async-start | bytes 8388608
  187.3 7.1 %slice-start.1 = ((s8[4227072]{0:T(1024)(128)(4,1)}), s8[32768]{0:T(1024)(128)(4,1)S(1)}, s32[]{:S(2)}) async-start(s8[4227072]{0:T(1024)(128)(4,1)} %bitcast.16), calls=%async_computation.1 | async-start | bytes 65536

commit v3 on v2

--- a/solution.py
+++ b/solution.py
@@ -22,6 +22,8 @@
 CH = 16
 NCH = NB // CH
 ROWS = CH * SEQ_LOC
+LATE = NCH - 1
+N_GAP = 3
 WCH = 4
 WROWS = D // WCH
 
@@ -41,11 +43,12 @@
 def kernel(lens, tab, g_attn, g_mlp,
            new_tok, prompt, w_q, w_k, w_v, w_o, w_g, w_u, w_d,
            o_last, o_dec, o_k, o_v,
-           buf_a, buf_b, buf_c, kv, stage, flat, q_buf, k_buf, v_buf, a_buf, att,
-           sel_r1, sel_r2, hid, normed, part, r1, r2, x2, mid, p_buf, out_buf, knv, rot, o_buf,
+           buf_a, buf_b, buf_c, kv, stage, stage_p, flat, q_buf, k_buf, v_buf, a_buf, att,
+           sel_r1, sel_r2, hid, normed, part, r1, r2, x2, mid, p_buf, knv, rot, o_buf,
+           rb, qb, qb_r, m_buf, l_buf, pb, pb_r,
            ld_p, ld_w, ld_big, st_sem,
            wp_s, wp_r, wx_s, wx_r, wfx_s, wfx_r, wy_s, wy_r, wfy_s, wfy_r,
-           sel_s, sel_r, kv_s, kv_r, ar_s, ar_r):
+           sel_s, sel_r, kv_s, kv_r, ar_s, ar_r, rb_s, rb_r, late_s, late_r, qp_s, qp_r):
     y = lax.axis_index("replica")
     m = lax.axis_index("model")
     c = lax.rem(m, 2)
@@ -171,11 +174,35 @@
 
     def kv_send(kind, h, j):
         dev = (pt, xs, xo)[kind]
-        return remote(stage.at[kind, h, j], kv_ref(h, j), kv_s.at[kind, h, j], kv_r.at[kind, h, j], dev)
+        return remote(stage_p.at[j] if kind == 0 else stage.at[kind - 1, h, j], kv_ref(h, j), kv_s.at[kind, h, j], kv_r.at[kind, h, j], dev)
+
+    def late_send(i):
+        kind, h, part8 = 1 + i % 2, (i // 2) % 2, i // 4
+        src = stage.at[kind - 1, h, LATE, pl.ds(part8 * 8, 8)]
+        dst = kv.at[h, pl.ds(LATE * CH + part8 * 8, 8), pl.ds(pl.multiple_of(m * 64, 64), 64)]
+        return remote(src, dst, late_s.at[i], late_r.at[i], (xs, xo)[i % 2])
+
+    my_rb = pl.ds(pl.multiple_of(c * 64, 64), 64)
+
+    def rb_send(h):
+        return remote(stage.at[1, h, LATE], rb.at[h, :, my_rb], rb_s.at[h], rb_r.at[h], pt)
+
+    def late_unit(h):
+        chunk = unit_chunk(xs_m, h, LATE)
+        stage[0, h, LATE] = chunk
+        rb[h, :, my_rb] = chunk
+        stage[1, h, LATE] = unit_chunk(xo_m, h, LATE)
+        rb_send(h).start()
 
     def run_unit(kind, h, j):
         owner = (pt_m, xs_m, xo_m)[kind]
-        stage[kind, h, j] = unit_chunk(owner, h, j)
+        chunk = unit_chunk(owner, h, j)
+        if kind == 0:
+            if h == 1:
+                kv_send(0, 0, j).wait_send()
+            stage_p[j] = chunk
+        else:
+            stage[kind - 1, h, j] = chunk
         kv_send(kind, h, j).start()
 
     def own_unit(h):
@@ -188,7 +215,7 @@
         def body(j, carry):
             run_unit(kind, h, j)
             return carry
-        lax.fori_loop(0, NCH, body, 0)
+        lax.fori_loop(0, NCH if kind == 0 else LATE, body, 0)
 
     forward_x(0)
     own_unit(0)
@@ -209,6 +236,7 @@
         wfx(r).wait_recv()
         wfy(r).wait_recv()
     loop_unit(2, 0)
+    late_unit(0)
     forward_x(3)
     forward_y(2)
     loop_unit(0, 1)
@@ -218,16 +246,6 @@
     s3 = remote(hid.at[half], hid.at[half], sel_s.at[2], sel_r.at[2], pt)
     s3.start()
     forward_y(3)
-    for r in range(2, WCH):
-        wfx(r).wait_recv()
-        wfy(r).wait_recv()
-
-    def last_units(j, carry):
-        run_unit(1, 1, j)
-        run_unit(2, 1, j)
-        return carry
-
-    lax.fori_loop(0, NCH, last_units, 0)
     s3.wait()
     load_t.wait()
 
@@ -282,6 +300,21 @@
     knv[0] = flat[0:2 * NB, :].astype(BF16)
     knv[1] = flat[2 * NB:4 * NB, :].astype(BF16)
 
+    qb[...] = q_buf[LATE * CH * 16:, :].astype(BF16)
+    q_msg = remote(qb, qb_r, qp_s.at[0], qp_r.at[0], xs)
+    q_msg.start()
+
+    for r in range(2, WCH):
+        wfx(r).wait_recv()
+        wfy(r).wait_recv()
+
+    def last_units(j, carry):
+        run_unit(1, 1, j)
+        run_unit(2, 1, j)
+        return carry
+
+    lax.fori_loop(0, LATE, last_units, 0)
+    late_unit(1)
     wp.wait_send()
     for r in range(WCH):
         wx(r).wait_send()
@@ -341,17 +374,82 @@
             return carry
         return body
 
-    for j in range(NCH):
+    c_half = lax.broadcasted_iota(jnp.int32, (16, 128), 1)
+    r_half = lax.broadcasted_iota(jnp.int32, (16, 128), 0)
+    same_half = ((r_half & 7) >= 3) == ((c_half & 1) == 1)
+    pos_half = x * 64 + (c_half >> 1)
+    on_diag = c_half == r_half
+    chip_rows = pl.ds(pl.multiple_of(x * 128, 128), 128)
+
+    def partial_scores(q, keys, b):
+        s = lax.dot_general(q, keys, (((1,), (1,)), ((), ())), preferred_element_type=F32) * scale
+        return jnp.where(same_half & (pos_half < lens[b]), s, NEG_BIG)
+
+    def late_local(p):
+        b = LATE * CH + p
+        rows = pl.ds(pl.multiple_of(b * 16, 16), 16)
+        out = pl.ds(pl.multiple_of(p * 16, 16), 16)
+        q = q_buf[rows, :]
+        s = partial_scores(q.astype(BF16), kv[0, b, chip_rows, :], b)
+        s_new = jnp.where(is_new, jnp.sum(q * k_buf[rows, :], axis=-1, keepdims=True) * scale, NEG_BIG)
+        top = jnp.maximum(jnp.max(s, axis=-1, keepdims=True), s_new)
+        w = jnp.exp(s - top)
+        w_new = jnp.exp(s_new - top)
+        m_buf[out, :] = jnp.broadcast_to(top, (16, HEAD_DIM))
+        l_buf[out, :] = jnp.broadcast_to(jnp.sum(w, axis=-1, keepdims=True) + w_new, (16, HEAD_DIM))
+        a_buf[rows, :] = dot32(w.astype(BF16), kv[1, b, chip_rows, :]) + w_new * v_buf[rows, :]
+
+    def late_peer(p):
+        out = pl.ds(pl.multiple_of(p * 16, 16), 16)
+        s = partial_scores(qb_r[out, :], rb[0, p], LATE * CH + p)
+        top = jnp.max(s, axis=-1, keepdims=True)
+        w = jnp.exp(s - top)
+        acc = dot32(w.astype(BF16), rb[1, p])
+        tops = jnp.sum(jnp.where(on_diag, top, 0.0), axis=0, keepdims=True)
+        sums = jnp.sum(jnp.where(on_diag, jnp.sum(w, axis=-1, keepdims=True), 0.0), axis=0, keepdims=True)
+        pb[out, :] = jnp.where(r_half == 6, tops, jnp.where(r_half == 7, sums, acc))
+
+    def late_merge(p):
+        rows = pl.ds(pl.multiple_of((LATE * CH + p) * 16, 16), 16)
+        out = pl.ds(pl.multiple_of(p * 16, 16), 16)
+        other = pb_r[out, :]
+        o_top = jnp.sum(jnp.where(on_diag, other[6:7, :], 0.0), axis=-1, keepdims=True)
+        o_sum = jnp.sum(jnp.where(on_diag, other[7:8, :], 0.0), axis=-1, keepdims=True)
+        top = jnp.maximum(m_buf[out, :], o_top)
+        w, o_w = jnp.exp(m_buf[out, :] - top), jnp.exp(o_top - top)
+        a_buf[rows, :] = (a_buf[rows, :] * w + other * o_w) / (l_buf[out, :] * w + o_sum * o_w)
+
+    def by_four(f):
+        def body(i, carry):
+            for t in range(4):
+                f(i * 4 + t)
+            return carry
+        lax.fori_loop(0, CH // 4, body, 0)
+
+    for j in range(LATE):
         for kind in range(3):
             kv_send(kind, 0, j).wait_recv()
         lax.fori_loop(j * (CH // 4), (j + 1) * (CH // 4), score_four, 0)
         lax.fori_loop(j * (CH // 8), (j + 1) * (CH // 8), lay_out(0), 0)
-    for j in range(NCH):
+    for h in range(2):
+        kv_send(0, h, LATE).wait_recv()
+        rb_send(h).wait_recv()
+    by_four(late_local)
+    q_msg.wait_recv()
+    by_four(late_peer)
+    p_msg = remote(pb, pb_r, qp_s.at[1], qp_r.at[1], xs)
+    p_msg.start()
+    for i in range(N_GAP):
+        late_send(i).start()
+
+    for j in range(LATE):
         for kind in range(3):
             kv_send(kind, 1, j).wait_recv()
         lax.fori_loop(j * (CH // 8), (j + 1) * (CH // 8), weigh_eight, 0)
-        if j < NCH - 1:
+        if j < LATE - 1:
             lax.fori_loop(j * (CH // 8), (j + 1) * (CH // 8), lay_out(1), 0)
+    p_msg.wait_recv()
+    by_four(late_merge)
 
     for hd in range(6):
         for t in range(2):
@@ -362,7 +460,7 @@
     mine_r1 = pl.ds(pl.multiple_of(x * 32, 32), 32)
     away_r1 = pl.ds(pl.multiple_of((1 - x) * 32, 32), 32)
 
-    def reduce_all(k, produce, after, resid, buf):
+    def reduce_all(k, produce, after, last, resid, buf):
         def msg(step, i, src, dst, dev):
             return remote(src, dst, ar_s.at[k, step, i], ar_r.at[k, step, i], dev)
 
@@ -392,6 +490,7 @@
             buf[mine, cols[i]] = (resid[mine, cols[i]].astype(F32) + total).astype(BF16)
             a3[i].start()
             a4[i].start()
+        last()
         for i in range(4):
             a3[i].wait_recv()
             a5[i].start()
@@ -408,9 +507,19 @@
 
     def after_w_o():
         load_u.start()
-        lax.fori_loop((NCH - 1) * (CH // 8), NB // 8, lay_out(1), 0)
-
-    reduce_all(0, w_o_cols, after_w_o, hid, x2)
+        lax.fori_loop((LATE - 1) * (CH // 8), LATE * (CH // 8), lay_out(1), 0)
+
+    def send_late():
+        for i in range(N_GAP, 8):
+            late_send(i).start()
+
+    def keep_late():
+        for i in range(8):
+            late_send(i).wait_recv()
+        for h in range(2):
+            lax.fori_loop(LATE * (CH // 8), NB // 8, lay_out(h), 0)
+
+    reduce_all(0, w_o_cols, after_w_o, send_late, hid, x2)
     gain_m = g_mlp[...].astype(F32)
 
     def norm_x2(i, carry):
@@ -439,20 +548,47 @@
             return carry
         lax.fori_loop(0, QW // 256, body, 0)
 
-    reduce_all(1, down_cols, lambda: None, x2, out_buf)
-    st_last = pltpu.make_async_copy(out_buf.at[pl.ds(0, NB)], o_last, st_sem.at[2])
-    st_dec = pltpu.make_async_copy(out_buf.at[pl.ds(NB, NB)], o_dec, st_sem.at[3])
+    reduce_all(1, down_cols, keep_late, lambda: None, x2, hid)
+    st_last = pltpu.make_async_copy(hid.at[pl.ds(0, NB)], o_last, st_sem.at[2])
+    st_dec = pltpu.make_async_copy(hid.at[pl.ds(NB, NB)], o_dec, st_sem.at[3])
     st_last.start()
     st_dec.start()
 
     for kind in range(3):
         for tn in range(2):
-            for j in range(NCH):
-                kv_send(kind, tn, j).wait_send()
+            for j in range(NCH if kind == 0 else LATE):
+                if kind or tn:
+                    kv_send(kind, tn, j).wait_send()
+    for i in range(8):
+        late_send(i).wait_send()
+    for h in range(2):
+        rb_send(h).wait_send()
+    q_msg.wait_send()
+    p_msg.wait_send()
     for h in range(2):
         store_kv(h, NB // 8 - 1).wait()
     st_last.wait()
     st_dec.wait()
+
+
+def copy_out(k_in, v_in, last_in, dec_in, k_out, v_out, last_out, dec_out, k_buf, v_buf, last_buf, dec_buf, rd, wr):
+    step = 8 * 258
+    moves = []
+    for i in range(NB // 8):
+        rows = pl.ds(i * step, step)
+        for src, buf, dst in ((k_in, k_buf, k_out), (v_in, v_buf, v_out)):
+            moves.append((src.at[rows], buf.at[rows], dst.at[rows]))
+    moves.append((last_in, last_buf, last_out))
+    moves.append((dec_in, dec_buf, dec_out))
+    reads = [pltpu.make_async_copy(a, b, rd.at[i]) for i, (a, b, _) in enumerate(moves)]
+    writes = [pltpu.make_async_copy(b, c, wr.at[i]) for i, (_, b, c) in enumerate(moves)]
+    for r in reads:
+        r.start()
+    for r, w in zip(reads, writes):
+        r.wait()
+        w.start()
+    for w in writes:
+        w.wait()
 
 
 def solution(mesh):
@@ -481,7 +617,8 @@
                 pltpu.VMEM((D, FF), BF16),
                 pltpu.VMEM((D, FF), BF16),
                 pltpu.VMEM((2, NB, 256, HEAD_DIM), BF16),
-                pltpu.VMEM((3, 2, NCH, CH, 64, HEAD_DIM), BF16),
+                pltpu.VMEM((2, 2, NCH, CH, 64, HEAD_DIM), BF16),
+                pltpu.VMEM((NCH, CH, 64, HEAD_DIM), BF16),
                 pltpu.VMEM((2 * ROWS, HEAD_DIM), F32),
                 pltpu.VMEM((NB * 16, HEAD_DIM), F32),
                 pltpu.VMEM((NB * 16, HEAD_DIM), F32),
@@ -498,19 +635,38 @@
                 pltpu.VMEM((2 * NB, D), BF16),
                 pltpu.VMEM((2 * NB, FF), BF16),
                 pltpu.VMEM((NB * 16, 256), BF16),
-                pltpu.VMEM((2 * NB, D), BF16),
                 pltpu.VMEM((2, 2 * NB, HEAD_DIM), BF16),
                 pltpu.VMEM((2, 2 * NB, HEAD_DIM), F32),
                 pltpu.VMEM((2, 8 * 258 + 32, HEAD_DIM), BF16),
+                pltpu.VMEM((2, CH, 128, HEAD_DIM), BF16),
+                pltpu.VMEM((CH * 16, HEAD_DIM), BF16),
+                pltpu.VMEM((CH * 16, HEAD_DIM), BF16),
+                pltpu.VMEM((CH * 16, HEAD_DIM), F32),
+                pltpu.VMEM((CH * 16, HEAD_DIM), F32),
+                pltpu.VMEM((CH * 16, HEAD_DIM), F32),
+                pltpu.VMEM((CH * 16, HEAD_DIM), F32),
                 dma((NCH,)), dma((2,)), dma((9,)), dma((4,)),
                 dma, dma, dma((WCH,)), dma((WCH,)), dma((WCH,)), dma((WCH,)),
                 dma((WCH,)), dma((WCH,)), dma((WCH,)), dma((WCH,)),
                 dma((3,)), dma((3,)), dma((3, 2, NCH)), dma((3, 2, NCH)), dma((2, 5, 4)), dma((2, 5, 4)),
+                dma((2,)), dma((2,)), dma((8,)), dma((8,)), dma((2,)), dma((2,)),
             ],
             compiler_params=pltpu.CompilerParams(collective_id=0, has_side_effects=True, vmem_limit_bytes=67043328),
             name="layer",
         )(lengths, tab, norm_attn, norm_mlp, new_tok,
           prompt.reshape(NB * SEQ_LOC, D), w_q[0], w_k[0], w_v[0], w_o[0], w_gate[0], w_up[0], w_down[0])
+        rows, slots = jax.ShapeDtypeStruct((NB, D), BF16), jax.ShapeDtypeStruct((NB * 258, HEAD_DIM), BF16)
+        n_moves = 2 * (NB // 8) + 2
+        o_k, o_v, o_last, o_dec = pl.pallas_call(
+            copy_out,
+            out_shape=(slots, slots, rows, rows),
+            in_specs=[hbm] * 4,
+            out_specs=(hbm,) * 4,
+            scratch_shapes=[pltpu.VMEM(slots.shape, BF16), pltpu.VMEM(slots.shape, BF16), pltpu.VMEM(rows.shape, BF16),
+                            pltpu.VMEM(rows.shape, BF16), dma((n_moves,)), dma((n_moves,))],
+            compiler_params=pltpu.CompilerParams(vmem_limit_bytes=60 * 1024 * 1024),
+            name="copy_out",
+        )(o_k, o_v, o_last, o_dec)
         caches = [o.reshape(1, NB, 129, 2, HEAD_DIM) for o in (o_k, o_v)]
         return o_dec, o_last, caches[0], caches[1]
 

time: 197 us -> 181 us (0.919)
  local copies, waits for them, and re-layouts: 12.8 us -> 0 us
  Pallas kernels: 183 us -> 180 us
    unnamed x8 -> x0, local copies, waits for them, and re-layouts: 12.8 us -> none
    pallas_call x1, Pallas kernels: 183 us -> 173 us  [per_device(): pl.pallas_call(kernel, out_shape=(jax.ShapeDtypeStruct((NB, D), BF16),) *...]
    pallas_call x0 -> x1, Pallas kernels: none -> 7.34 us  [per_device(): pl.pallas_call(copy_out, out_shape=(slots, slots, rows, rows), in_specs=[...]
where the time goes in v3:
time: 181 us
  Pallas kernels  180 us (99%)
    pallas_call x1, Pallas kernels, per_device(): pl.pallas_call(kernel, out_shape=(jax.ShapeDtypeStruct((NB, D), BF16),) *...  173 us
    pallas_call x1, Pallas kernels, per_device(): pl.pallas_call(copy_out, out_shape=(slots, slots, rows, rows), in_specs=[...  7.34 us

profile of v3, /device:TPU:0, one launch (start us, length us, event | category | flops | bytes accessed | tf_op | source)
XLA Modules:
  0.0 181.2 jit_solution(4969989058151853700)
XLA Ops:
  0.6 173.0 %layer.1 = (bf16[64,3072]{1,0:T(8,128)(2,1)}, bf16[64,3072]{1,0:T(8,128)(2,1)}, bf16[16512,128]{1,0:T(8,128)(2,1)}, bf16[16512,128]{1,0:T(8,128)(2,1)}) custom-call(s32[64]{0:T(128)} %lens.1, f32[2,136,128]{2,1,0:T(8,128)} %constant.2.clone.tab, bf16[1,3072]{1,0:T(2,128)(2,1)} %g_attn.1, bf16[1,3072]{1,0:T(2,128)(2,1)} %g_mlp.1, bf16[64,3072]{1,0:T(8,128)(2,1)} %new_tok.1, ...), custom_call_target="tpu_custom_call" | custom-call | tf_op jit(solution)/shard_map/layer/pallas_call | solution.py:610
  173.7 7.3 %copy_out.1 = (bf16[16512,128]{1,0:T(8,128)(2,1)}, bf16[16512,128]{1,0:T(8,128)(2,1)}, bf16[64,3072]{1,0:T(8,128)(2,1)}, bf16[64,3072]{1,0:T(8,128)(2,1)}) custom-call(bf16[16512,128]{1,0:T(8,128)(2,1)} %get-tuple-element.12.k_in, bf16[16512,128]{1,0:T(8,128)(2,1)} %get-tuple-element.13.v_in, bf16[64,3072]{1,0:T(8,128)(2,1)} %get-tuple-element.14.last_in, ...), custom_call_target="tpu_custom_call" | custom-call | tf_op jit(solution)/shard_map/copy_out/pallas_call | solution.py:660

commit v4 on v3

--- a/solution.py
+++ b/solution.py
@@ -22,6 +22,7 @@
 CH = 16
 NCH = NB // CH
 ROWS = CH * SEQ_LOC
+VMEM_LAYER = 67043328 - (10 << 20)
 LATE = NCH - 1
 N_GAP = 3
 WCH = 4
@@ -42,11 +43,11 @@
 
 def kernel(lens, tab, g_attn, g_mlp,
            new_tok, prompt, w_q, w_k, w_v, w_o, w_g, w_u, w_d,
-           o_last, o_dec, o_k, o_v,
-           buf_a, buf_b, buf_c, kv, stage, stage_p, flat, q_buf, k_buf, v_buf, a_buf, att,
-           sel_r1, sel_r2, hid, normed, part, r1, r2, x2, mid, p_buf, knv, rot, o_buf,
+           kv, knv, hid,
+           buf_a, buf_b, buf_c, stage, stage_p, flat, q_buf, k_buf, v_buf, a_buf, att,
+           sel_r1, sel_r2, normed, part, r1, r2, x2, mid, p_buf, rot,
            rb, qb, qb_r, m_buf, l_buf, pb, pb_r,
-           ld_p, ld_w, ld_big, st_sem,
+           ld_p, ld_w, ld_big,
            wp_s, wp_r, wx_s, wx_r, wfx_s, wfx_r, wy_s, wy_r, wfy_s, wfy_r,
            sel_s, sel_r, kv_s, kv_r, ar_s, ar_r, rb_s, rb_r, late_s, late_r, qp_s, qp_r):
     y = lax.axis_index("replica")
@@ -356,24 +357,6 @@
             a_buf[rows, :] = a_buf[rows, :] + dot32(p_buf[rows, :], kv[1, b])
         return carry
 
-    def store_kv(h, g):
-        rows = pl.ds(pl.multiple_of(g * 2064, 2064), 2064)
-        return pltpu.make_async_copy(o_buf.at[h, pl.ds(0, 2064)], (o_k, o_v)[h].at[rows], st_sem.at[h])
-
-    def lay_out(h):
-        def body(g, carry):
-            @pl.when(g > 0)
-            def _():
-                store_kv(h, g - 1).wait()
-            for t in range(8):
-                o_buf[h, t * 258:t * 258 + 256, :] = kv[h, g * 8 + t]
-            new = knv[h, pl.ds(pl.multiple_of(g * 16, 16), 16), :]
-            for t in range(8):
-                o_buf[h, t * 258 + 256:t * 258 + 258, :] = new[2 * t:2 * t + 2]
-            store_kv(h, g).start()
-            return carry
-        return body
-
     c_half = lax.broadcasted_iota(jnp.int32, (16, 128), 1)
     r_half = lax.broadcasted_iota(jnp.int32, (16, 128), 0)
     same_half = ((r_half & 7) >= 3) == ((c_half & 1) == 1)
@@ -430,7 +413,6 @@
         for kind in range(3):
             kv_send(kind, 0, j).wait_recv()
         lax.fori_loop(j * (CH // 4), (j + 1) * (CH // 4), score_four, 0)
-        lax.fori_loop(j * (CH // 8), (j + 1) * (CH // 8), lay_out(0), 0)
     for h in range(2):
         kv_send(0, h, LATE).wait_recv()
         rb_send(h).wait_recv()
@@ -446,8 +428,6 @@
         for kind in range(3):
             kv_send(kind, 1, j).wait_recv()
         lax.fori_loop(j * (CH // 8), (j + 1) * (CH // 8), weigh_eight, 0)
-        if j < LATE - 1:
-            lax.fori_loop(j * (CH // 8), (j + 1) * (CH // 8), lay_out(1), 0)
     p_msg.wait_recv()
     by_four(late_merge)
 
@@ -507,7 +487,6 @@
 
     def after_w_o():
         load_u.start()
-        lax.fori_loop((LATE - 1) * (CH // 8), LATE * (CH // 8), lay_out(1), 0)
 
     def send_late():
         for i in range(N_GAP, 8):
@@ -516,8 +495,6 @@
     def keep_late():
         for i in range(8):
             late_send(i).wait_recv()
-        for h in range(2):
-            lax.fori_loop(LATE * (CH // 8), NB // 8, lay_out(h), 0)
 
     reduce_all(0, w_o_cols, after_w_o, send_late, hid, x2)
     gain_m = g_mlp[...].astype(F32)
@@ -549,11 +526,6 @@
         lax.fori_loop(0, QW // 256, body, 0)
 
     reduce_all(1, down_cols, keep_late, lambda: None, x2, hid)
-    st_last = pltpu.make_async_copy(hid.at[pl.ds(0, NB)], o_last, st_sem.at[2])
-    st_dec = pltpu.make_async_copy(hid.at[pl.ds(NB, NB)], o_dec, st_sem.at[3])
-    st_last.start()
-    st_dec.start()
-
     for kind in range(3):
         for tn in range(2):
             for j in range(NCH if kind == 0 else LATE):
@@ -565,30 +537,38 @@
         rb_send(h).wait_send()
     q_msg.wait_send()
     p_msg.wait_send()
-    for h in range(2):
-        store_kv(h, NB // 8 - 1).wait()
-    st_last.wait()
-    st_dec.wait()
-
-
-def copy_out(k_in, v_in, last_in, dec_in, k_out, v_out, last_out, dec_out, k_buf, v_buf, last_buf, dec_buf, rd, wr):
-    step = 8 * 258
-    moves = []
-    for i in range(NB // 8):
-        rows = pl.ds(i * step, step)
-        for src, buf, dst in ((k_in, k_buf, k_out), (v_in, v_buf, v_out)):
-            moves.append((src.at[rows], buf.at[rows], dst.at[rows]))
-    moves.append((last_in, last_buf, last_out))
-    moves.append((dec_in, dec_buf, dec_out))
-    reads = [pltpu.make_async_copy(a, b, rd.at[i]) for i, (a, b, _) in enumerate(moves)]
-    writes = [pltpu.make_async_copy(b, c, wr.at[i]) for i, (_, b, c) in enumerate(moves)]
-    for r in reads:
+
+
+def copy_out(kv, knv, hid, k_out, v_out, last_out, dec_out, buf, sem, row_sem):
+    rows = [pltpu.make_async_copy(hid.at[pl.ds(i * NB, NB)], dst, row_sem.at[i]) for i, dst in enumerate((last_out, dec_out))]
+    for r in rows:
         r.start()
-    for r, w in zip(reads, writes):
+
+    def store(h, g):
+        dst = pl.ds(pl.multiple_of(g * 2064, 2064), 2064)
+        slot = lax.rem(g, 2)
+        return pltpu.make_async_copy(buf.at[h, slot, pl.ds(0, 2064)], (k_out, v_out)[h].at[dst], sem.at[h, slot])
+
+    def lay_out(g, carry):
+        slot = lax.rem(g, 2)
+        for h in range(2):
+            @pl.when(g > 1)
+            def _():
+                store(h, g - 2).wait()
+            for t in range(8):
+                buf[h, slot, t * 258:t * 258 + 256, :] = kv[h, g * 8 + t]
+            new = knv[h, pl.ds(pl.multiple_of(g * 16, 16), 16), :]
+            for t in range(8):
+                buf[h, slot, t * 258 + 256:t * 258 + 258, :] = new[2 * t:2 * t + 2]
+            store(h, g).start()
+        return carry
+
+    lax.fori_loop(0, NB // 8, lay_out, 0)
+    for g in range(NB // 8 - 2, NB // 8):
+        for h in range(2):
+            store(h, g).wait()
+    for r in rows:
         r.wait()
-        w.start()
-    for w in writes:
-        w.wait()
 
 
 def solution(mesh):
@@ -607,16 +587,15 @@
         hbm = pl.BlockSpec(memory_space=pl.ANY)
         smem = pl.BlockSpec(memory_space=pltpu.SMEM)
         dma = pltpu.SemaphoreType.DMA
-        o_last, o_dec, o_k, o_v = pl.pallas_call(
+        kv, knv, hid = pl.pallas_call(
             kernel,
-            out_shape=(jax.ShapeDtypeStruct((NB, D), BF16),) * 2 + (jax.ShapeDtypeStruct((NB * 258, HEAD_DIM), BF16),) * 2,
+            out_shape=(pltpu.VMEM((2, NB, 256, HEAD_DIM), BF16), pltpu.VMEM((2, 2 * NB, HEAD_DIM), BF16), pltpu.VMEM((2 * NB, D), BF16)),
             in_specs=[smem] + [vmem] * 3 + [hbm] * 9,
-            out_specs=(hbm,) * 4,
+            out_specs=(vmem,) * 3,
             scratch_shapes=[
                 pltpu.VMEM((NB * SEQ_LOC, D), BF16),
                 pltpu.VMEM((D, FF), BF16),
                 pltpu.VMEM((D, FF), BF16),
-                pltpu.VMEM((2, NB, 256, HEAD_DIM), BF16),
                 pltpu.VMEM((2, 2, NCH, CH, 64, HEAD_DIM), BF16),
                 pltpu.VMEM((NCH, CH, 64, HEAD_DIM), BF16),
                 pltpu.VMEM((2 * ROWS, HEAD_DIM), F32),
@@ -628,16 +607,13 @@
                 pltpu.VMEM((NB, D), BF16),
                 pltpu.VMEM((32, D), BF16),
                 pltpu.VMEM((2 * NB, D), BF16),
-                pltpu.VMEM((2 * NB, D), BF16),
                 pltpu.VMEM((2 * NB, D), F32),
                 pltpu.VMEM((NB, D), F32),
                 pltpu.VMEM((32, D), F32),
                 pltpu.VMEM((2 * NB, D), BF16),
                 pltpu.VMEM((2 * NB, FF), BF16),
                 pltpu.VMEM((NB * 16, 256), BF16),
-                pltpu.VMEM((2, 2 * NB, HEAD_DIM), BF16),
                 pltpu.VMEM((2, 2 * NB, HEAD_DIM), F32),
-                pltpu.VMEM((2, 8 * 258 + 32, HEAD_DIM), BF16),
                 pltpu.VMEM((2, CH, 128, HEAD_DIM), BF16),
                 pltpu.VMEM((CH * 16, HEAD_DIM), BF16),
                 pltpu.VMEM((CH * 16, HEAD_DIM), BF16),
@@ -645,28 +621,26 @@
                 pltpu.VMEM((CH * 16, HEAD_DIM), F32),
                 pltpu.VMEM((CH * 16, HEAD_DIM), F32),
                 pltpu.VMEM((CH * 16, HEAD_DIM), F32),
-                dma((NCH,)), dma((2,)), dma((9,)), dma((4,)),
+                dma((NCH,)), dma((2,)), dma((9,)),
                 dma, dma, dma((WCH,)), dma((WCH,)), dma((WCH,)), dma((WCH,)),
                 dma((WCH,)), dma((WCH,)), dma((WCH,)), dma((WCH,)),
                 dma((3,)), dma((3,)), dma((3, 2, NCH)), dma((3, 2, NCH)), dma((2, 5, 4)), dma((2, 5, 4)),
                 dma((2,)), dma((2,)), dma((8,)), dma((8,)), dma((2,)), dma((2,)),
             ],
-            compiler_params=pltpu.CompilerParams(collective_id=0, has_side_effects=True, vmem_limit_bytes=67043328),
+            compiler_params=pltpu.CompilerParams(collective_id=0, has_side_effects=True, vmem_limit_bytes=VMEM_LAYER),
             name="layer",
         )(lengths, tab, norm_attn, norm_mlp, new_tok,
           prompt.reshape(NB * SEQ_LOC, D), w_q[0], w_k[0], w_v[0], w_o[0], w_gate[0], w_up[0], w_down[0])
         rows, slots = jax.ShapeDtypeStruct((NB, D), BF16), jax.ShapeDtypeStruct((NB * 258, HEAD_DIM), BF16)
-        n_moves = 2 * (NB // 8) + 2
         o_k, o_v, o_last, o_dec = pl.pallas_call(
             copy_out,
             out_shape=(slots, slots, rows, rows),
-            in_specs=[hbm] * 4,
+            in_specs=[vmem] * 3,
             out_specs=(hbm,) * 4,
-            scratch_shapes=[pltpu.VMEM(slots.shape, BF16), pltpu.VMEM(slots.shape, BF16), pltpu.VMEM(rows.shape, BF16),
-                            pltpu.VMEM(rows.shape, BF16), dma((n_moves,)), dma((n_moves,))],
-            compiler_params=pltpu.CompilerParams(vmem_limit_bytes=60 * 1024 * 1024),
+            scratch_shapes=[pltpu.VMEM((2, 2, 8 * 258 + 32, HEAD_DIM), BF16), dma((2, 2)), dma((2,))],
+            compiler_params=pltpu.CompilerParams(vmem_limit_bytes=40 << 20),
             name="copy_out",
-        )(o_k, o_v, o_last, o_dec)
+        )(kv, knv, hid)
         caches = [o.reshape(1, NB, 129, 2, HEAD_DIM) for o in (o_k, o_v)]
         return o_dec, o_last, caches[0], caches[1]
 

time: 181 us -> 177 us (0.978)
  Pallas kernels: 180 us -> 177 us
    pallas_call x1, Pallas kernels: 7.34 us -> 4.37 us  [per_device(): pl.pallas_call(copy_out, out_shape=(slots, slots, rows, rows), in_specs=[...]
where the time goes in v4:
time: 177 us
  Pallas kernels  177 us (100%)
    pallas_call x1, Pallas kernels, per_device(): pl.pallas_call(kernel, out_shape=(pltpu.VMEM((2, NB, 256, HEAD_DIM), BF16...  172 us
    pallas_call x1, Pallas kernels, per_device(): pl.pallas_call(copy_out, out_shape=(slots, slots, rows, rows), in_specs=[...  4.37 us

profile of v4, /device:TPU:0, one launch (start us, length us, event | category | flops | bytes accessed | tf_op | source)
XLA Modules:
  0.0 177.3 jit_solution(8420641027238837161)
XLA Ops:
  0.6 172.2 %layer.1 = (bf16[2,64,256,128]{3,2,1,0:T(8,128)(2,1)S(1)}, bf16[2,128,128]{2,1,0:T(8,128)(2,1)S(1)}, bf16[128,3072]{1,0:T(8,128)(2,1)S(1)}) custom-call(s32[64]{0:T(128)} %lens.1, f32[2,136,128]{2,1,0:T(8,128)} %constant.2.clone.tab, bf16[1,3072]{1,0:T(2,128)(2,1)} %g_attn.1, bf16[1,3072]{1,0:T(2,128)(2,1)} %g_mlp.1, bf16[64,3072]{1,0:T(8,128)(2,1)} %new_tok.1, ...), custom_call_target="tpu_custom_call" | custom-call | tf_op jit(solution)/shard_map/layer/pallas_call | solution.py:590
  172.8 4.4 %copy_out.1 = (bf16[16512,128]{1,0:T(8,128)(2,1)}, bf16[16512,128]{1,0:T(8,128)(2,1)}, bf16[64,3072]{1,0:T(8,128)(2,1)}, bf16[64,3072]{1,0:T(8,128)(2,1)}) custom-call(bf16[2,64,256,128]{3,2,1,0:T(8,128)(2,1)S(1)} %get-tuple-element.11.kv, bf16[2,128,128]{2,1,0:T(8,128)(2,1)S(1)} %get-tuple-element.12.knv, bf16[128,3072]{1,0:T(8,128)(2,1)S(1)} %get-tuple-element.13.hid), custom_call_target="tpu_custom_call" | custom-call | tf_op jit(solution)/shard_map/copy_out/pallas_call | solution.py:635

commit v5 on v4

--- a/solution.py
+++ b/solution.py
@@ -24,7 +24,9 @@
 ROWS = CH * SEQ_LOC
 VMEM_LAYER = 67043328 - (10 << 20)
 LATE = NCH - 1
-N_GAP = 3
+N_LATE = 16
+N_GAP = 4
+N_MID = 1
 WCH = 4
 WROWS = D // WCH
 
@@ -41,13 +43,13 @@
     return np.stack([np.concatenate([cos_tab, cos_tab], 1), np.concatenate([-sin_tab, sin_tab], 1)]).astype(np.float32)
 
 
-def kernel(lens, tab, g_attn, g_mlp,
+def kernel(lens, tab_in, g_attn_in, g_mlp_in,
            new_tok, prompt, w_q, w_k, w_v, w_o, w_g, w_u, w_d,
            kv, knv, hid,
            buf_a, buf_b, buf_c, stage, stage_p, flat, q_buf, k_buf, v_buf, a_buf, att,
            sel_r1, sel_r2, normed, part, r1, r2, x2, mid, p_buf, rot,
-           rb, qb, qb_r, m_buf, l_buf, pb, pb_r,
-           ld_p, ld_w, ld_big,
+           tab, g_attn, g_mlp, rb, qb, qb_r, m_buf, l_buf, pb, pb_r,
+           ld_p, ld_w, ld_big, ld_small,
            wp_s, wp_r, wx_s, wx_r, wfx_s, wfx_r, wy_s, wy_r, wfy_s, wfy_r,
            sel_s, sel_r, kv_s, kv_r, ar_s, ar_r, rb_s, rb_r, late_s, late_r, qp_s, qp_r):
     y = lax.axis_index("replica")
@@ -79,6 +81,10 @@
     load_q.start()
     load_t = pltpu.make_async_copy(new_tok, hid.at[pl.ds(NB, NB)], ld_big.at[8])
     load_t.start()
+    small = [pltpu.make_async_copy(src, dst, ld_small.at[i])
+             for i, (src, dst) in enumerate(((tab_in, tab), (g_attn_in, g_attn), (g_mlp_in, g_mlp)))]
+    for cp in small:
+        cp.start()
 
     def load_o(i):
         return pltpu.make_async_copy(w_o.at[:, pl.ds(i * QW, QW)], buf_c.at[pl.ds(i * QW, QW), pl.ds(QW, QW)], ld_big.at[1 + i])
@@ -99,8 +105,8 @@
         return buf_b.at[rows, pl.ds(pl.multiple_of(owner * 512 + (r // 2) * 256, 256), 256)]
 
     def wx(r):
-        ref = w_ref(m, y, r)
-        return remote(ref, ref, wx_s.at[r], wx_r.at[r], xs)
+        src = (w_k, w_v)[r // 2].at[pl.ds(pl.multiple_of(y * (D // 2) + (r % 2) * WROWS, WROWS), WROWS)]
+        return remote(src, w_ref(m, y, r), wx_s.at[r], wx_r.at[r], xs)
 
     def wfx(r):
         ref = w_ref(xs_m, y, r)
@@ -116,10 +122,10 @@
 
     own = buf_b.at[:, pl.ds(pl.multiple_of(m * 512, 512), 512)]
     wp = remote(own, own, wp_s, wp_r, pt)
+    for r in range(WCH):
+        wx(r).start()
     for i in range(2):
         load_w(i).wait()
-    for r in range(WCH):
-        wx(r).start()
     wp.start()
 
     def forward_x(r):
@@ -131,6 +137,8 @@
         wy(r).wait_recv()
         wfy(r).start()
 
+    for cp in small:
+        cp.wait()
     gain_a = g_attn[...].astype(F32)
     row_iota = lax.broadcasted_iota(jnp.int32, (SEQ_LOC, 1), 0)
 
@@ -178,9 +186,9 @@
         return remote(stage_p.at[j] if kind == 0 else stage.at[kind - 1, h, j], kv_ref(h, j), kv_s.at[kind, h, j], kv_r.at[kind, h, j], dev)
 
     def late_send(i):
-        kind, h, part8 = 1 + i % 2, (i // 2) % 2, i // 4
-        src = stage.at[kind - 1, h, LATE, pl.ds(part8 * 8, 8)]
-        dst = kv.at[h, pl.ds(LATE * CH + part8 * 8, 8), pl.ds(pl.multiple_of(m * 64, 64), 64)]
+        kind, h, first = 1 + i % 2, (i // 2) % 2, i // 4 * 4
+        src = stage.at[kind - 1, h, LATE, pl.ds(first, 4)]
+        dst = kv.at[h, pl.ds(LATE * CH + first, 4), pl.ds(pl.multiple_of(m * 64, 64), 64)]
         return remote(src, dst, late_s.at[i], late_r.at[i], (xs, xo)[i % 2])
 
     my_rb = pl.ds(pl.multiple_of(c * 64, 64), 64)
@@ -465,6 +473,9 @@
         over_x(3)
         after()
         for i in range(4):
+            if i == 3:
+                for t in range(N_MID):
+                    late_send((N_GAP, N_LATE - N_MID)[k] + t).start()
             a2[i].wait_recv()
             total = part[mine, cols[i]] + r2[:, cols[i]]
             buf[mine, cols[i]] = (resid[mine, cols[i]].astype(F32) + total).astype(BF16)
@@ -489,11 +500,11 @@
         load_u.start()
 
     def send_late():
-        for i in range(N_GAP, 8):
+        for i in range(N_GAP + N_MID, N_LATE - N_MID):
             late_send(i).start()
 
     def keep_late():
-        for i in range(8):
+        for i in range(N_LATE - N_MID):
             late_send(i).wait_recv()
 
     reduce_all(0, w_o_cols, after_w_o, send_late, hid, x2)
@@ -531,8 +542,10 @@
             for j in range(NCH if kind == 0 else LATE):
                 if kind or tn:
                     kv_send(kind, tn, j).wait_send()
-    for i in range(8):
+    for i in range(N_LATE):
         late_send(i).wait_send()
+    for i in range(N_LATE - N_MID, N_LATE):
+        late_send(i).wait_recv()
     for h in range(2):
         rb_send(h).wait_send()
     q_msg.wait_send()
@@ -590,7 +603,7 @@
         kv, knv, hid = pl.pallas_call(
             kernel,
             out_shape=(pltpu.VMEM((2, NB, 256, HEAD_DIM), BF16), pltpu.VMEM((2, 2 * NB, HEAD_DIM), BF16), pltpu.VMEM((2 * NB, D), BF16)),
-            in_specs=[smem] + [vmem] * 3 + [hbm] * 9,
+            in_specs=[smem] + [hbm] * 12,
             out_specs=(vmem,) * 3,
             scratch_shapes=[
                 pltpu.VMEM((NB * SEQ_LOC, D), BF16),
@@ -614,6 +627,9 @@
                 pltpu.VMEM((2 * NB, FF), BF16),
                 pltpu.VMEM((NB * 16, 256), BF16),
                 pltpu.VMEM((2, 2 * NB, HEAD_DIM), F32),
+                pltpu.VMEM((2, 136, HEAD_DIM), F32),
+                pltpu.VMEM((1, D), BF16),
+                pltpu.VMEM((1, D), BF16),
                 pltpu.VMEM((2, CH, 128, HEAD_DIM), BF16),
                 pltpu.VMEM((CH * 16, HEAD_DIM), BF16),
                 pltpu.VMEM((CH * 16, HEAD_DIM), BF16),
@@ -621,11 +637,11 @@
                 pltpu.VMEM((CH * 16, HEAD_DIM), F32),
                 pltpu.VMEM((CH * 16, HEAD_DIM), F32),
                 pltpu.VMEM((CH * 16, HEAD_DIM), F32),
-                dma((NCH,)), dma((2,)), dma((9,)),
+                dma((NCH,)), dma((2,)), dma((9,)), dma((3,)),
                 dma, dma, dma((WCH,)), dma((WCH,)), dma((WCH,)), dma((WCH,)),
                 dma((WCH,)), dma((WCH,)), dma((WCH,)), dma((WCH,)),
                 dma((3,)), dma((3,)), dma((3, 2, NCH)), dma((3, 2, NCH)), dma((2, 5, 4)), dma((2, 5, 4)),
-                dma((2,)), dma((2,)), dma((8,)), dma((8,)), dma((2,)), dma((2,)),
+                dma((2,)), dma((2,)), dma((N_LATE,)), dma((N_LATE,)), dma((2,)), dma((2,)),
             ],
             compiler_params=pltpu.CompilerParams(collective_id=0, has_side_effects=True, vmem_limit_bytes=VMEM_LAYER),
             name="layer",

time: 177 us -> 172 us (0.972)
  Pallas kernels: 177 us -> 171 us
    pallas_call x1, Pallas kernels: 172 us -> 166 us  [per_device(): pl.pallas_call(kernel, out_shape=(pltpu.VMEM((2, NB, 256, HEAD_DIM), BF16...]
where the time goes in v5:
time: 172 us; the launch traced here: 171 us
  Pallas kernels  171 us (99%)
    pallas_call x1, Pallas kernels, per_device(): pl.pallas_call(kernel, out_shape=(pltpu.VMEM((2, NB, 256, HEAD_DIM), BF16...  166 us
    pallas_call x1, Pallas kernels, per_device(): pl.pallas_call(copy_out, out_shape=(slots, slots, rows, rows), in_specs=[...  4.37 us

profile of v5, /device:TPU:0, one launch (start us, length us, event | category | flops | bytes accessed | tf_op | source)
XLA Modules:
  0.0 171.4 jit_solution(302781843688446621)
XLA Ops:
  0.6 166.3 %layer.1 = (bf16[2,64,256,128]{3,2,1,0:T(8,128)(2,1)S(1)}, bf16[2,128,128]{2,1,0:T(8,128)(2,1)S(1)}, bf16[128,3072]{1,0:T(8,128)(2,1)S(1)}) custom-call(s32[64]{0:T(128)} %lens.1, f32[2,136,128]{2,1,0:T(8,128)} %constant.2.clone.tab_in, bf16[1,3072]{1,0:T(2,128)(2,1)} %g_attn_in.1, bf16[1,3072]{1,0:T(2,128)(2,1)} %g_mlp_in.1, bf16[64,3072]{1,0:T(8,128)(2,1)} %new_tok.1, ...), custom_call_target="tpu_custom_call" | custom-call | tf_op jit(solution)/shard_map/layer/pallas_call | solution.py:603
  166.9 4.4 %copy_out.1 = (bf16[16512,128]{1,0:T(8,128)(2,1)}, bf16[16512,128]{1,0:T(8,128)(2,1)}, bf16[64,3072]{1,0:T(8,128)(2,1)}, bf16[64,3072]{1,0:T(8,128)(2,1)}) custom-call(bf16[2,64,256,128]{3,2,1,0:T(8,128)(2,1)S(1)} %get-tuple-element.11.kv, bf16[2,128,128]{2,1,0:T(8,128)(2,1)S(1)} %get-tuple-element.12.knv, bf16[128,3072]{1,0:T(8,128)(2,1)S(1)} %get-tuple-element.13.hid), custom_call_target="tpu_custom_call" | custom-call | tf_op jit(solution)/shard_map/copy_out/pallas_call | solution.py:651

commit v6 on v5

--- a/solution.py
+++ b/solution.py
@@ -24,9 +24,11 @@
 ROWS = CH * SEQ_LOC
 VMEM_LAYER = 67043328 - (10 << 20)
 LATE = NCH - 1
+N_EARLY = 1
 N_LATE = 16
 N_GAP = 4
-N_MID = 1
+N_MID = 0
+N_FIRST = 4 * N_EARLY + N_GAP
 WCH = 4
 WROWS = D // WCH
 
@@ -202,6 +204,9 @@
         rb[h, :, my_rb] = chunk
         stage[1, h, LATE] = unit_chunk(xo_m, h, LATE)
         rb_send(h).start()
+        for t in range(N_EARLY):
+            for i in range(2):
+                late_send(4 * t + 2 * h + i).start()
 
     def run_unit(kind, h, j):
         owner = (pt_m, xs_m, xo_m)[kind]
@@ -310,7 +315,8 @@
     knv[1] = flat[2 * NB:4 * NB, :].astype(BF16)
 
     qb[...] = q_buf[LATE * CH * 16:, :].astype(BF16)
-    q_msg = remote(qb, qb_r, qp_s.at[0], qp_r.at[0], xs)
+    late_rows = pl.ds(N_EARLY * 64, CH * 16 - N_EARLY * 64)
+    q_msg = remote(qb.at[late_rows], qb_r.at[late_rows], qp_s.at[0], qp_r.at[0], xs)
     q_msg.start()
 
     for r in range(2, WCH):
@@ -358,11 +364,13 @@
             score(i * 4 + t)
         return carry
 
+    def weigh(b):
+        rows = pl.ds(pl.multiple_of(b * 16, 16), 16)
+        a_buf[rows, :] = a_buf[rows, :] + dot32(p_buf[rows, :], kv[1, b])
+
     def weigh_eight(i, carry):
         for t in range(8):
-            b = i * 8 + t
-            rows = pl.ds(pl.multiple_of(b * 16, 16), 16)
-            a_buf[rows, :] = a_buf[rows, :] + dot32(p_buf[rows, :], kv[1, b])
+            weigh(i * 8 + t)
         return carry
 
     c_half = lax.broadcasted_iota(jnp.int32, (16, 128), 1)
@@ -415,7 +423,7 @@
             for t in range(4):
                 f(i * 4 + t)
             return carry
-        lax.fori_loop(0, CH // 4, body, 0)
+        lax.fori_loop(N_EARLY, CH // 4, body, 0)
 
     for j in range(LATE):
         for kind in range(3):
@@ -424,18 +432,27 @@
     for h in range(2):
         kv_send(0, h, LATE).wait_recv()
         rb_send(h).wait_recv()
+    for t in range(N_EARLY):
+        for i in range(2):
+            late_send(4 * t + i).wait_recv()
+        score_four(LATE * (CH // 4) + t, 0)
     by_four(late_local)
     q_msg.wait_recv()
     by_four(late_peer)
-    p_msg = remote(pb, pb_r, qp_s.at[1], qp_r.at[1], xs)
+    p_msg = remote(pb.at[late_rows], pb_r.at[late_rows], qp_s.at[1], qp_r.at[1], xs)
     p_msg.start()
-    for i in range(N_GAP):
+    for i in range(4 * N_EARLY, N_FIRST):
         late_send(i).start()
 
     for j in range(LATE):
         for kind in range(3):
             kv_send(kind, 1, j).wait_recv()
         lax.fori_loop(j * (CH // 8), (j + 1) * (CH // 8), weigh_eight, 0)
+    for t in range(N_EARLY):
+        for i in range(2):
+            late_send(4 * t + 2 + i).wait_recv()
+        for b in range(LATE * CH + 4 * t, LATE * CH + 4 * t + 4):
+            weigh(b)
     p_msg.wait_recv()
     by_four(late_merge)
 
@@ -475,7 +492,7 @@
         for i in range(4):
             if i == 3:
                 for t in range(N_MID):
-                    late_send((N_GAP, N_LATE - N_MID)[k] + t).start()
+                    late_send((N_FIRST, N_LATE - N_MID)[k] + t).start()
             a2[i].wait_recv()
             total = part[mine, cols[i]] + r2[:, cols[i]]
             buf[mine, cols[i]] = (resid[mine, cols[i]].astype(F32) + total).astype(BF16)
@@ -500,11 +517,11 @@
         load_u.start()
 
     def send_late():
-        for i in range(N_GAP + N_MID, N_LATE - N_MID):
+        for i in range(N_FIRST + N_MID, N_LATE - N_MID):
             late_send(i).start()
 
     def keep_late():
-        for i in range(N_LATE - N_MID):
+        for i in range(4 * N_EARLY, N_LATE - N_MID):
             late_send(i).wait_recv()
 
     reduce_all(0, w_o_cols, after_w_o, send_late, hid, x2)

time: 172 us -> 170 us (0.988)
  no operation moved by 1% of the time
where the time goes in v6:
time: 170 us
  Pallas kernels  170 us (100%)
    pallas_call x1, Pallas kernels, per_device(): pl.pallas_call(kernel, out_shape=(pltpu.VMEM((2, NB, 256, HEAD_DIM), BF16...  165 us
    pallas_call x1, Pallas kernels, per_device(): pl.pallas_call(copy_out, out_shape=(slots, slots, rows, rows), in_specs=[...  4.37 us

profile of v6, /device:TPU:0, one launch (start us, length us, event | category | flops | bytes accessed | tf_op | source)
XLA Modules:
  0.0 170.4 jit_solution(6618164901108816017)
XLA Ops:
  0.6 165.2 %layer.1 = (bf16[2,64,256,128]{3,2,1,0:T(8,128)(2,1)S(1)}, bf16[2,128,128]{2,1,0:T(8,128)(2,1)S(1)}, bf16[128,3072]{1,0:T(8,128)(2,1)S(1)}) custom-call(s32[64]{0:T(128)} %lens.1, f32[2,136,128]{2,1,0:T(8,128)} %constant.2.clone.tab_in, bf16[1,3072]{1,0:T(2,128)(2,1)} %g_attn_in.1, bf16[1,3072]{1,0:T(2,128)(2,1)} %g_mlp_in.1, bf16[64,3072]{1,0:T(8,128)(2,1)} %new_tok.1, ...), custom_call_target="tpu_custom_call" | custom-call | tf_op jit(solution)/shard_map/layer/pallas_call | solution.py:620
  165.8 4.4 %copy_out.1 = (bf16[16512,128]{1,0:T(8,128)(2,1)}, bf16[16512,128]{1,0:T(8,128)(2,1)}, bf16[64,3072]{1,0:T(8,128)(2,1)}, bf16[64,3072]{1,0:T(8,128)(2,1)}) custom-call(bf16[2,64,256,128]{3,2,1,0:T(8,128)(2,1)S(1)} %get-tuple-element.11.kv, bf16[2,128,128]{2,1,0:T(8,128)(2,1)S(1)} %get-tuple-element.12.knv, bf16[128,3072]{1,0:T(8,128)(2,1)S(1)} %get-tuple-element.13.hid), custom_call_target="tpu_custom_call" | custom-call | tf_op jit(solution)/shard_map/copy_out/pallas_call | solution.py:668

commit v7 on v6

--- a/solution.py
+++ b/solution.py
@@ -575,26 +575,26 @@
         r.start()
 
     def store(h, g):
-        dst = pl.ds(pl.multiple_of(g * 2064, 2064), 2064)
-        slot = lax.rem(g, 2)
-        return pltpu.make_async_copy(buf.at[h, slot, pl.ds(0, 2064)], (k_out, v_out)[h].at[dst], sem.at[h, slot])
+        dst = pl.ds(pl.multiple_of(g * 1032, 8), 1032)
+        slot = lax.rem(g, 4)
+        return pltpu.make_async_copy(buf.at[h, slot, pl.ds(0, 1032)], (k_out, v_out)[h].at[dst], sem.at[h, slot])
 
     def lay_out(g, carry):
-        slot = lax.rem(g, 2)
+        slot = lax.rem(g, 4)
         for h in range(2):
-            @pl.when(g > 1)
+            @pl.when(g > 3)
             def _():
-                store(h, g - 2).wait()
-            for t in range(8):
-                buf[h, slot, t * 258:t * 258 + 256, :] = kv[h, g * 8 + t]
-            new = knv[h, pl.ds(pl.multiple_of(g * 16, 16), 16), :]
-            for t in range(8):
+                store(h, g - 4).wait()
+            for t in range(4):
+                buf[h, slot, t * 258:t * 258 + 256, :] = kv[h, g * 4 + t]
+            new = knv[h, pl.ds(pl.multiple_of(g * 8, 8), 8), :]
+            for t in range(4):
                 buf[h, slot, t * 258 + 256:t * 258 + 258, :] = new[2 * t:2 * t + 2]
             store(h, g).start()
         return carry
 
-    lax.fori_loop(0, NB // 8, lay_out, 0)
-    for g in range(NB // 8 - 2, NB // 8):
+    lax.fori_loop(0, NB // 4, lay_out, 0)
+    for g in range(NB // 4 - 4, NB // 4):
         for h in range(2):
             store(h, g).wait()
     for r in rows:
@@ -670,7 +670,7 @@
             out_shape=(slots, slots, rows, rows),
             in_specs=[vmem] * 3,
             out_specs=(hbm,) * 4,
-            scratch_shapes=[pltpu.VMEM((2, 2, 8 * 258 + 32, HEAD_DIM), BF16), dma((2, 2)), dma((2,))],
+            scratch_shapes=[pltpu.VMEM((2, 4, 4 * 258 + 40, HEAD_DIM), BF16), dma((2, 4)), dma((2,))],
             compiler_params=pltpu.CompilerParams(vmem_limit_bytes=40 << 20),
             name="copy_out",
         )(kv, knv, hid)

time: 170 us -> 170 us (level)
  no operation moved by 1% of the time
where the time goes in v7:
time: 170 us
  Pallas kernels  169 us (99%)
    pallas_call x1, Pallas kernels, per_device(): pl.pallas_call(kernel, out_shape=(pltpu.VMEM((2, NB, 256, HEAD_DIM), BF16...  165 us
    pallas_call x1, Pallas kernels, per_device(): pl.pallas_call(copy_out, out_shape=(slots, slots, rows, rows), in_specs=[...  3.95 us

profile of v7, /device:TPU:0, one launch (start us, length us, event | category | flops | bytes accessed | tf_op | source)
XLA Modules:
  0.0 170.0 jit_solution(12140951232850280745)
XLA Ops:
  0.6 165.2 %layer.1 = (bf16[2,64,256,128]{3,2,1,0:T(8,128)(2,1)S(1)}, bf16[2,128,128]{2,1,0:T(8,128)(2,1)S(1)}, bf16[128,3072]{1,0:T(8,128)(2,1)S(1)}) custom-call(s32[64]{0:T(128)} %lens.1, f32[2,136,128]{2,1,0:T(8,128)} %constant.2.clone.tab_in, bf16[1,3072]{1,0:T(2,128)(2,1)} %g_attn_in.1, bf16[1,3072]{1,0:T(2,128)(2,1)} %g_mlp_in.1, bf16[64,3072]{1,0:T(8,128)(2,1)} %new_tok.1, ...), custom_call_target="tpu_custom_call" | custom-call | tf_op jit(solution)/shard_map/layer/pallas_call | solution.py:620
  165.8 4.0 %copy_out.1 = (bf16[16512,128]{1,0:T(8,128)(2,1)}, bf16[16512,128]{1,0:T(8,128)(2,1)}, bf16[64,3072]{1,0:T(8,128)(2,1)}, bf16[64,3072]{1,0:T(8,128)(2,1)}) custom-call(bf16[2,64,256,128]{3,2,1,0:T(8,128)(2,1)S(1)} %get-tuple-element.11.kv, bf16[2,128,128]{2,1,0:T(8,128)(2,1)S(1)} %get-tuple-element.12.knv, bf16[128,3072]{1,0:T(8,128)(2,1)S(1)} %get-tuple-element.13.hid), custom_call_target="tpu_custom_call" | custom-call | tf_op jit(solution)/shard_map/copy_out/pallas_call | solution.py:668
